TPU v7x, 128 devices: a whole 4x4x4 slice. The times are simulated.
128 devices in a mesh: rep: 1, r: 4 (over x), s: 32 (over y, z, core).
Axes of the slice: x: 4, y: 4, z: 4, core: 2. Of those that a mesh axis runs over, the one named last changes fastest.
Arguments:
- x: bfloat16 [128, 2048, 1024], P(('rep', 'r', 's'))
- dy: bfloat16 [128, 2048, 1024], P(('rep', 'r', 's'))
- w_gate: bfloat16 [2, 1024, 3584], P(None, 's')
- w_up: bfloat16 [2, 1024, 3584], P(None, 's')
- w_down: bfloat16 [2, 3584, 1024], P(None, 's')
- m_w_gate: float32 [2, 1024, 3584], P(None, 's')
- m_w_up: float32 [2, 1024, 3584], P(None, 's')
- m_w_down: float32 [2, 3584, 1024], P(None, 's')
- v_w_gate: float32 [2, 1024, 3584], P(None, 's')
- v_w_up: float32 [2, 1024, 3584], P(None, 's')
- v_w_down: float32 [2, 3584, 1024], P(None, 's')
Outputs:
- output 1: bfloat16 [2, 1024, 3584], P('rep', 's')
- output 2: bfloat16 [2, 1024, 3584], P('rep', 's')
- output 3: bfloat16 [2, 3584, 1024], P('rep', 's')
- output 4: float32 [2, 1024, 3584], P('rep', 's')
- output 5: float32 [2, 1024, 3584], P('rep', 's')
- output 6: float32 [2, 3584, 1024], P('rep', 's')
- output 7: float32 [2, 1024, 3584], P('rep', 's')
- output 8: float32 [2, 1024, 3584], P('rep', 's')
- output 9: float32 [2, 3584, 1024], P('rep', 's')
All inputs are finite; a program needn't handle non-finite values.
Results may differ from a plain program's by a relative error of at most 0.022.
Values are sent between devices in bfloat16 or wider.
A program may use at most 1.5 GiB of HBM per device.

v0:
```python
import jax
import jax.numpy as jnp
from jax import lax
from jax.sharding import PartitionSpec as P

NAMES = ("w_gate", "w_up", "w_down")


def matmul(a, w):
    return jnp.dot(a, w, preferred_element_type=jnp.float32).astype(jnp.bfloat16)


def normed(h):
    wide = h.astype(jnp.float32)
    scale = lax.rsqrt(jnp.mean(wide**2, -1, keepdims=True) + 1e-6)
    return (wide * scale).astype(jnp.bfloat16)


def layer(h, w):
    a = normed(h)
    gate = jnp.dot(a, w["w_gate"], preferred_element_type=jnp.float32)
    up = jnp.dot(a, w["w_up"], preferred_element_type=jnp.float32)
    return h + matmul((jax.nn.silu(gate) * up).astype(jnp.bfloat16), w["w_down"])


def adamw(w, m, v, g):
    m = 0.9 * m + 0.1 * g
    v = 0.95 * v + 0.05 * g * g
    step = m * lax.rsqrt(v + 1e-8) + 0.1 * w
    return (w - 0.02 * step).astype(jnp.bfloat16), m, v


def solution(mesh):
    def fetched(weights, number):
        return {name: lax.all_gather(w[number], "s", axis=0, tiled=True) for name, w in zip(NAMES, weights, strict=True)}

    def summed(term):
        return lax.psum(lax.psum_scatter(term, "s", scatter_dimension=0, tiled=True), "r")

    def step(x, dy, *arrays):
        weights, m, v = (arrays[i : i + 3] for i in (0, 3, 6))
        layers = weights[0].shape[0]
        h, kept = x[0], []
        for number in range(layers):
            kept.append(h)
            h = layer(h, fetched(weights, number))
        by_h, mine = dy[0], [None] * layers
        for number in reversed(range(layers)):
            _, back = jax.vjp(lambda w, h: layer(h, w), fetched(weights, number), kept[number])
            by_w, by_h = back(by_h)
            mine[number] = [summed(by_w[name]) for name in NAMES]
        gradients = [jnp.stack([mine[number][i] for number in range(layers)]).astype(jnp.float32) for i in range(3)]
        new = [adamw(w.astype(jnp.float32), m, v, g) for w, m, v, g in zip(weights, m, v, gradients, strict=True)]
        return tuple(one[which] for which in range(3) for one in new)

    states, cut = P(("rep", "r", "s"), None, None), P(None, "s", None)
    return jax.shard_map(
        step,
        mesh=mesh,
        in_specs=(states, states) + (cut,) * 9,
        out_specs=(P("rep", "s", None),) * 9,
        check_vma=False,
    )
```

profile of v0, /device:TPU:1, one launch (start us, length us, event | category | flops | bytes accessed | tf_op | source)
XLA Modules:
  0.0 1054.6 jit_solution(15640625844363841976)
XLA Ops:
  30.8 34.5 %all-gather.13.cloned.1.call-done = bf16[1,1024,3584]{2,1,0:T(8,128)(2,1)} async-done(((bf16[1,32,3584]{2,1,0:T(8,128)(2,1)}), bf16[1,1024,3584]{2,1,0:T(8,128)(2,1)}) %all-gather.13.cloned.1.call-update) | async-done | bytes 7340048 | tf_op jit(solution)/shard_map/all_gather | solution.py:35
  65.3 24.2 %fusion.41 = f32[2048,3584]{1,0:T(8,128)} fusion(bf16[1,1024,3584]{2,1,0:T(8,128)(2,1)} %all-gather.13.cloned.1.call-done, bf16[1,2048,1024]{1,2,0:T(8,128)(2,1)} %copy.20, f32[2048]{0:T(1024)S(1)} %add_rsqrt_fusion), kind=kOutput, calls=%fused_computation.59 | convolution fusion | flops 15038676992 | bytes 40902656 | tf_op jit(solution)/shard_map/dot_general | solution.py:21
  89.5 28.3 %all-gather.15.cloned.1.call-done = bf16[1,1024,3584]{2,1,0:T(8,128)(2,1)} async-done(((bf16[1,32,3584]{2,1,0:T(8,128)(2,1)}), bf16[1,1024,3584]{2,1,0:T(8,128)(2,1)}) %all-gather.15.cloned.1.call-update) | async-done | bytes 7340048 | tf_op jit(solution)/shard_map/all_gather | solution.py:35
  117.8 34.8 %multiply_convert_fusion.1 = (bf16[2048,3584]{1,0:T(8,128)(2,1)}, f32[2048,3584]{1,0:T(8,128)}) fusion(f32[2048,3584]{1,0:T(8,128)} %fusion.41, bf16[1,1024,3584]{2,1,0:T(8,128)(2,1)} %all-gather.15.cloned.1.call-done, bf16[1,2048,1024]{1,2,0:T(8,128)(2,1)} %copy.20, f32[2048]{0:T(1024)S(1)} %add_rsqrt_fusion), kind=kOutput, calls=%fused_computation.17 | convolution fusion | flops 15082717184 | bytes 84942848 | tf_op jit(solution)/shard_map/dot_general | solution.py:22
  170.3 21.9 %fusion.19 = (f32[2048]{0:T(1024)S(1)}, bf16[2048,1024]{0,1:T(8,128)(2,1)}) fusion(bf16[2048,3584]{1,0:T(8,128)(2,1)} %get-tuple-element.30, bf16[1,3584,1024]{2,1,0:T(8,128)(2,1)} %all-gather.17.cloned.1.call-done, bf16[1,2048,1024]{1,2,0:T(8,128)(2,1)} %copy.20), kind=kOutput, calls=%fused_computation.37 | convolution fusion | flops 15042869248 | bytes 30416896 | tf_op jit(solution)/shard_map/dot_general | solution.py:10
  192.9 29.8 %all-gather.21.cloned.1.call-done = bf16[1,3584,1024]{2,1,0:T(8,128)(2,1)} async-done(((bf16[1,112,1024]{2,1,0:T(8,128)(2,1)}), bf16[1,3584,1024]{2,1,0:T(8,128)(2,1)}) %all-gather.21.cloned.1.call-update) | async-done | bytes 7340048 | tf_op jit(solution)/shard_map/all_gather | solution.py:35
  222.7 22.3 %convolution_convert_fusion.1 = bf16[2048,3584]{1,0:T(8,128)(2,1)} fusion(bf16[1,3584,1024]{2,1,0:T(8,128)(2,1)} %all-gather.21.cloned.1.call-done, bf16[1,2048,1024]{2,1,0:T(8,128)(2,1)} %param.12), kind=kOutput, calls=%fused_computation.23 | convolution fusion | flops 15039725568 | bytes 26214400 | tf_op jit(solution)/shard_map/transpose(jvp())/dot_general | solution.py:10
  245.0 30.1 %all-gather.23.cloned.1.call-done = bf16[1,1024,3584]{2,1,0:T(8,128)(2,1)} async-done(((bf16[1,32,3584]{2,1,0:T(8,128)(2,1)}), bf16[1,1024,3584]{2,1,0:T(8,128)(2,1)}) %all-gather.23.cloned.1.call-update) | async-done | bytes 7340048 | tf_op jit(solution)/shard_map/all_gather | solution.py:35
  275.1 24.5 %fusion.28 = f32[2048,3584]{1,0:T(8,128)} fusion(bf16[1,1024,3584]{2,1,0:T(8,128)(2,1)} %all-gather.23.cloned.1.call-done, bf16[2048,1024]{0,1:T(8,128)(2,1)} %get-tuple-element.33, f32[2048]{0:T(1024)S(1)} %fusion.74), kind=kOutput, calls=%fused_computation.46 | convolution fusion | flops 15038676992 | bytes 40902656 | tf_op jit(solution)/shard_map/jvp()/dot_general | solution.py:22
  299.6 27.9 %all-gather.19.cloned.1.call-done = bf16[1,1024,3584]{2,1,0:T(8,128)(2,1)} async-done(((bf16[1,32,3584]{2,1,0:T(8,128)(2,1)}), bf16[1,1024,3584]{2,1,0:T(8,128)(2,1)}) %all-gather.19.cloned.1.call-update) | async-done | bytes 7340048 | tf_op jit(solution)/shard_map/all_gather | solution.py:35
  327.5 43.4 %fusion.2 = (bf16[2048,3584]{1,0:T(8,128)(2,1)}, f32[2048,3584]{1,0:T(8,128)}) fusion(f32[2048,3584]{1,0:T(8,128)} %fusion.28, bf16[2048,3584]{1,0:T(8,128)(2,1)} %convolution_convert_fusion.1, bf16[1,1024,3584]{2,1,0:T(8,128)(2,1)} %all-gather.19.cloned.1.call-done, bf16[2048,1024]{0,1:T(8,128)(2,1)} %get-tuple-element.33, f32[2048]{0:T(1024)S(1)} %fusion.74), kind=kOutput, calls=%fused_computation.8 | convolution fusion | flops 15126757376 | bytes 99622912 | tf_op jit(solution)/shard_map/jvp()/dot_general | solution.py:21
  370.9 24.3 %fusion.12 = bf16[2048,1024]{0,1:T(8,128)(2,1)} fusion(bf16[2048,3584]{1,0:T(8,128)(2,1)} %convolution_convert_fusion.1, bf16[1,1024,3584]{2,1,0:T(8,128)(2,1)} %all-gather.23.cloned.1.call-done, f32[2048,3584]{1,0:T(8,128)} %get-tuple-element.35), kind=kOutput, calls=%fused_computation.21 | convolution fusion | flops 15076425728 | bytes 55574528 | tf_op jit(solution)/shard_map/transpose(jvp())/dot_general | solution.py:22
  395.2 22.3 %fusion.21 = (f32[2048]{0:T(1024)S(1)}, bf16[2048,1024]{0,1:T(8,128)(2,1)}) fusion(bf16[2048,1024]{0,1:T(8,128)(2,1)S(1)} %copy-done.1, bf16[2048,1024]{0,1:T(8,128)(2,1)} %fusion.12, bf16[2048,3584]{1,0:T(8,128)(2,1)} %get-tuple-element.34, bf16[1,1024,3584]{2,1,0:T(8,128)(2,1)} %all-gather.19.cloned.1.call-done), kind=kOutput, calls=%fused_computation.39 | convolution fusion | flops 15042869248 | bytes 34611200 | tf_op jit(solution)/shard_map/transpose(jvp())/dot_general | solution.py:21
  445.1 27.4 %fusion.25 = bf16[3584,1024]{1,0:T(8,128)(2,1)} fusion(f32[2048,3584]{1,0:T(8,128)} %fusion.28, bf16[1,2048,1024]{2,1,0:T(8,128)(2,1)} %param.12, f32[2048,3584]{1,0:T(8,128)} %get-tuple-element.35), kind=kOutput, calls=%fused_computation.41 | convolution fusion | flops 15080095744 | bytes 70254592 | tf_op jit(solution)/shard_map/transpose(jvp())/dot_general | solution.py:10
  472.6 22.4 %convolution_convert_fusion = bf16[2048,3584]{1,0:T(8,128)(2,1)} fusion(bf16[2048,1024]{0,1:T(8,128)(2,1)} %copy-done.2, bf16[1,3584,1024]{2,1,0:T(8,128)(2,1)} %all-gather.17.cloned.1.call-done), kind=kOutput, calls=%fused_computation.22 | convolution fusion | flops 15039725568 | bytes 26214400 | tf_op jit(solution)/shard_map/transpose(jvp())/dot_general | solution.py:10
  494.9 26.2 %fusion.27 = bf16[1024,3584]{1,0:T(8,128)(2,1)} fusion(bf16[2048,3584]{1,0:T(8,128)(2,1)} %convolution_convert_fusion, f32[2048,3584]{1,0:T(8,128)} %fusion.41, bf16[1,2048,1024]{1,2,0:T(8,128)(2,1)} %copy.20, f32[2048]{0:T(1024)S(1)} %copy-done.13), kind=kOutput, calls=%fused_computation.43 | convolution fusion | flops 15086387200 | bytes 55582720 | tf_op jit(solution)/shard_map/transpose(jvp())/dot_general | solution.py:22
  521.2 25.8 %fusion.26 = bf16[1024,3584]{1,0:T(8,128)(2,1)} fusion(bf16[2048,3584]{1,0:T(8,128)(2,1)} %convolution_convert_fusion.1, bf16[2048,1024]{0,1:T(8,128)(2,1)} %get-tuple-element.33, f32[2048]{0:T(1024)S(1)} %copy-done.9, f32[2048,3584]{1,0:T(8,128)} %get-tuple-element.35), kind=kOutput, calls=%fused_computation.42 | convolution fusion | flops 15086387200 | bytes 55582720 | tf_op jit(solution)/shard_map/transpose(jvp())/dot_general | solution.py:22
  547.1 34.2 %fusion.22 = bf16[1024,3584]{1,0:T(8,128)(2,1)} fusion(f32[2048,3584]{1,0:T(8,128)} %fusion.41, f32[2048,3584]{1,0:T(8,128)} %get-tuple-element.31, bf16[2048,3584]{1,0:T(8,128)(2,1)} %convolution_convert_fusion, bf16[1,2048,1024]{1,2,0:T(8,128)(2,1)} %copy.20, f32[2048]{0:T(1024)S(1)} %copy-done.13), kind=kOutput, calls=%fused_computation.40 | convolution fusion | flops 15123087360 | bytes 84942848 | tf_op jit(solution)/shard_map/transpose(jvp())/dot_general | solution.py:21
  581.3 21.7 %convolution_convert_fusion.3 = bf16[1024,3584]{1,0:T(8,128)(2,1)} fusion(bf16[2048,3584]{1,0:T(8,128)(2,1)} %get-tuple-element.34, bf16[2048,1024]{0,1:T(8,128)(2,1)} %get-tuple-element.33, f32[2048]{0:T(1024)S(1)} %copy-done.9), kind=kOutput, calls=%fused_computation.45 | convolution fusion | flops 15038676992 | bytes 26222592 | tf_op jit(solution)/shard_map/transpose(jvp())/dot_general | solution.py:21
  622.2 91.6 %reduce-scatter.11.cloned.1.call-done = bf16[32,3584]{1,0:T(8,128)(2,1)} async-done(((bf16[1024,3584]{1,0:T(8,128)(2,1)}), bf16[32,3584]{1,0:T(8,128)(2,1)}) %reduce-scatter.11.cloned.1.call-update) | async-done | bytes 229392 | tf_op jit(solution)/shard_map/reduce_scatter | solution.py:38
  713.8 91.5 %reduce-scatter.13.cloned.1.call-done = bf16[32,3584]{1,0:T(8,128)(2,1)} async-done(((bf16[1024,3584]{1,0:T(8,128)(2,1)}), bf16[32,3584]{1,0:T(8,128)(2,1)}) %reduce-scatter.13.cloned.1.call-update) | async-done | bytes 229392 | tf_op jit(solution)/shard_map/reduce_scatter | solution.py:38
  805.3 91.7 %reduce-scatter.7.cloned.1.call-done = bf16[32,3584]{1,0:T(8,128)(2,1)} async-done(((bf16[1024,3584]{1,0:T(8,128)(2,1)}), bf16[32,3584]{1,0:T(8,128)(2,1)}) %reduce-scatter.7.cloned.1.call-update) | async-done | bytes 229392 | tf_op jit(solution)/shard_map/reduce_scatter | solution.py:38
  897.0 91.4 %reduce-scatter.9.cloned.1.call-done = bf16[32,3584]{1,0:T(8,128)(2,1)} async-done(((bf16[1024,3584]{1,0:T(8,128)(2,1)}), bf16[32,3584]{1,0:T(8,128)(2,1)}) %reduce-scatter.9.cloned.1.call-update) | async-done | bytes 229392 | tf_op jit(solution)/shard_map/reduce_scatter | solution.py:38
  988.4 51.6 %all-reduce.3.cloned.1.call-done = (bf16[1,32,3584]{2,1,0:T(8,128)(2,1)}, bf16[1,32,3584]{2,1,0:T(8,128)(2,1)}, bf16[1,32,3584]{2,1,0:T(8,128)(2,1)}, bf16[1,32,...) async-done(((bf16[1,32,3584]{2,1,0:T(8,128)(2,1)}, bf16[1,32,3584]{2,1,0:T(8,128)(2,1)}, bf16[1,32,3584]{2,1,0:T(8,128)(2,1)}, ...) | async-done | bytes 1376272 | tf_op jit(solution)/shard_map/psum | solution.py:38
  (70 shorter events, 96.7 us)
Async XLA Ops:
  7.2 58.1 %all-gather.13.cloned.1.call-start = ((), (), s32[]{:S(2)}) async-start(), calls=%async_computation.12 | async-start | bytes 7569408 | tf_op jit(solution)/shard_map/all_gather | solution.py:35
  9.1 108.7 %all-gather.15.cloned.1.call-start = ((), (), s32[]{:S(2)}) async-start(), calls=%async_computation.13 | async-start | bytes 7569408 | tf_op jit(solution)/shard_map/all_gather | solution.py:35
  11.0 159.3 %all-gather.17.cloned.1.call-start = ((), (), s32[]{:S(2)}) async-start(), calls=%async_computation.14 | async-start | bytes 7569408 | tf_op jit(solution)/shard_map/all_gather | solution.py:35
  12.9 209.8 %all-gather.21.cloned.1.call-start = ((), (), s32[]{:S(2)}) async-start(), calls=%async_computation.16 | async-start | bytes 7569408 | tf_op jit(solution)/shard_map/all_gather | solution.py:35
  13.5 261.6 %all-gather.23.cloned.1.call-start = ((), (), s32[]{:S(2)}) async-start(), calls=%async_computation.17 | async-start | bytes 7569408 | tf_op jit(solution)/shard_map/all_gather | solution.py:35
  14.1 313.4 %all-gather.19.cloned.1.call-start = ((), (), s32[]{:S(2)}) async-start(), calls=%async_computation.15 | async-start | bytes 7569408 | tf_op jit(solution)/shard_map/all_gather | solution.py:35
  14.7 588.5 %reduce-scatter.15.cloned.1.call-start = ((), (), s32[]{:S(2)}) async-start(), calls=%async_computation.10 | async-start | bytes 7569408 | tf_op jit(solution)/shard_map/reduce_scatter | solution.py:38
  24.3 93.5 %copy-start.12 = (f32[2048]{0:T(1024)}, f32[2048]{0:T(1024)S(1)}, u32[]{:S(2)}) copy-start(f32[2048]{0:T(1024)S(1)} %add_rsqrt_fusion) | copy-start | bytes 24580
  192.9 224.6 %copy-start.8 = (f32[2048]{0:T(1024)}, f32[2048]{0:T(1024)S(1)}, u32[]{:S(2)}) copy-start(f32[2048]{0:T(1024)S(1)} %fusion.74) | copy-start | bytes 24580
  370.9 24.3 %copy-start.1 = (bf16[2048,1024]{0,1:T(8,128)(2,1)S(1)}, bf16[2048,1024]{0,1:T(8,128)(2,1)}, u32[]{:S(2)}) copy-start(bf16[2048,1024]{0,1:T(8,128)(2,1)} %get-tuple-element.33) | copy-start | bytes 12582916
  395.2 22.3 %copy-start = (bf16[1,2048,1024]{1,2,0:T(8,128)(2,1)S(1)}, bf16[1,2048,1024]{1,2,0:T(8,128)(2,1)}, u32[]{:S(2)}) copy-start(bf16[1,2048,1024]{1,2,0:T(8,128)(2,1)} %copy.21) | copy-start | bytes 12582916
  445.0 177.1 %reduce-scatter.17.cloned.1.call-start = ((), (), s32[]{:S(2)}) async-start(), calls=%async_computation.11 | async-start | bytes 7569408 | tf_op jit(solution)/shard_map/reduce_scatter | solution.py:38
  472.5 22.4 %copy-start.13 = (f32[2048]{0:T(1024)S(1)}, f32[2048]{0:T(1024)}, u32[]{:S(2)}) copy-start(f32[2048]{0:T(1024)} %copy-done.12) | copy-start | bytes 24580
  472.5 241.3 %reduce-scatter.11.cloned.1.call-start = ((), (), s32[]{:S(2)}) async-start(), calls=%async_computation.8 | async-start | bytes 7569408 | tf_op jit(solution)/shard_map/reduce_scatter | solution.py:38
  494.9 26.2 %copy-start.9 = (f32[2048]{0:T(1024)S(1)}, f32[2048]{0:T(1024)}, u32[]{:S(2)}) copy-start(f32[2048]{0:T(1024)} %copy-done.8) | copy-start | bytes 24580
  521.1 284.2 %reduce-scatter.13.cloned.1.call-start = ((), (), s32[]{:S(2)}) async-start(), calls=%async_computation.9 | async-start | bytes 7569408 | tf_op jit(solution)/shard_map/reduce_scatter | solution.py:38
  547.0 349.9 %reduce-scatter.7.cloned.1.call-start = ((), (), s32[]{:S(2)}) async-start(), calls=%async_computation.6 | async-start | bytes 7569408 | tf_op jit(solution)/shard_map/reduce_scatter | solution.py:38
  581.3 407.1 %reduce-scatter.9.cloned.1.call-start = ((), (), s32[]{:S(2)}) async-start(), calls=%async_computation.7 | async-start | bytes 7569408 | tf_op jit(solution)/shard_map/reduce_scatter | solution.py:38
  603.0 437.0 %copy-start.3 = (bf16[2,112,1024]{2,1,0:T(8,128)(2,1)S(1)}, bf16[2,112,1024]{2,1,0:T(8,128)(2,1)}, u32[]{:S(2)}) copy-start(bf16[2,112,1024]{2,1,0:T(8,128)(2,1)} %param.15) | copy-start | bytes 1376260
  603.0 440.4 %copy-start.4 = (bf16[2,32,3584]{2,1,0:T(8,128)(2,1)S(1)}, bf16[2,32,3584]{2,1,0:T(8,128)(2,1)}, u32[]{:S(2)}) copy-start(bf16[2,32,3584]{2,1,0:T(8,128)(2,1)} %param.13) | copy-start | bytes 1376260
  603.0 440.4 %copy-start.5 = (bf16[2,32,3584]{2,1,0:T(8,128)(2,1)S(1)}, bf16[2,32,3584]{2,1,0:T(8,128)(2,1)}, u32[]{:S(2)}) copy-start(bf16[2,32,3584]{2,1,0:T(8,128)(2,1)} %param.14) | copy-start | bytes 1376260
  603.0 440.4 %copy-start.6 = (f32[2,32,3584]{2,1,0:T(8,128)S(1)}, f32[2,32,3584]{2,1,0:T(8,128)}, u32[]{:S(2)}) copy-start(f32[2,32,3584]{2,1,0:T(8,128)} %param.19) | copy-start | bytes 2752516
  603.0 440.4 %copy-start.7 = (f32[2,32,3584]{2,1,0:T(8,128)S(1)}, f32[2,32,3584]{2,1,0:T(8,128)}, u32[]{:S(2)}) copy-start(f32[2,32,3584]{2,1,0:T(8,128)} %param.16) | copy-start | bytes 2752516
  603.1 436.9 %all-reduce.3.cloned.1.call-start = ((), (), s32[]{:S(2)}) async-start(), calls=%async_computation.18 | async-start | bytes 2752512 | tf_op jit(solution)/shard_map/psum | solution.py:38
  (3 other events, 24.9 us)
Sparse Core Ops, SparseCore 0:
  10.8 54.4 all-gather.12
  68.1 49.6 all-gather.14
  120.6 49.6 all-gather.16
  173.0 49.6 all-gather.20
  225.4 49.6 all-gather.22
  277.8 49.6 all-gather.18
  445.2 85.2 reduce-scatter.14
  534.2 87.8 reduce-scatter.16
  625.9 87.7 reduce-scatter.10
  717.4 87.8 reduce-scatter.12
  809.1 87.8 reduce-scatter.6
  900.6 87.7 reduce-scatter.8
  991.1 48.8 all-reduce.2
where the time goes:
time: 1060 us; the launch traced here: 1050 us
  waiting for transfers between devices  607 us (57%)
  matrix products  396 us (37%)
  local copies, waits for them, and re-layouts  21.2 us (2%)
  other arithmetic  15.8 us (1%)
  between operations  14.2 us (1%)
    reduce_scatter x6, waiting for transfers between devices, summed(): lax.psum_scatter(term, 's', scatter_dimension=0, tiled=True)  385 us
    all_gather x6, waiting for transfers between devices, fetched(): lax.all_gather(w[number], 's', axis=0, tiled=True)  168 us
    dot_general x5, matrix products, layer(): gate = jnp.dot(a, w['w_gate'], preferred_element_type=jnp.float32)  146 us
    dot_general x5, matrix products, layer(): up = jnp.dot(a, w['w_up'], preferred_element_type=jnp.float32)  136 us
    dot_general x5, matrix products, matmul(): jnp.dot(a, w, preferred_element_type=jnp.float32).astype(jnp.bfloat16)  115 us
    psum x1, waiting for transfers between devices, summed(): lax.psum(lax.psum_scatter(term, 's', scatter_dimension=0, tiled=True), 'r')  51.6 us
  transfers between devices with their start and end apart: 13, of which 12 were waited for; matrix products, arithmetic and copies ran while one was open for 29% of the time, Pallas kernels for 0%

commit v1 on v0

v1 whole, which is shorter than its diff:
```python
import functools

import jax
import jax.numpy as jnp
from jax import lax
from jax.experimental import pallas as pl
from jax.experimental.pallas import tpu as pltpu
from jax.sharding import PartitionSpec as P

BF, F32 = jnp.bfloat16, jnp.float32
MESH = pl.DeviceIdType.MESH
ANY = pl.BlockSpec(memory_space=pl.ANY)
TT, UU, VV = 0, 1, 2


def place():
    s = lax.axis_index("s")
    return lax.axis_index("r"), s // 8, (s // 2) % 4, s % 2


def at_s(y, z, c):
    return {"s": (y * 4 + z) * 2 + c}


def step_to(k, d):
    return lax.rem(k + d + 4, 4)


def mate(order, which, d):
    _, y, z, c = place()
    along_y = (order == 0) == (which == 0)
    return at_s(step_to(y, d), z, c) if along_y else at_s(y, step_to(z, d), c)


def partner():
    _, y, z, c = place()
    return at_s(y, z, 1 - c)


def remote(src, dst, send, recv, to):
    return pltpu.make_async_remote_copy(src_ref=src, dst_ref=dst, send_sem=send, recv_sem=recv, device_id=to, device_id_type=MESH)


class Gather:
    far = False

    def __init__(self, order, shard):
        self.order = order
        rows, cols = shard.shape
        self.rows, self.cols = rows, cols
        self.inputs = [shard]
        self.outs = [jax.ShapeDtypeStruct((4, 4, 2, rows, cols), BF)]
        self.out_specs = [ANY]
        self.scratch = [pltpu.VMEM((rows, cols), BF), pltpu.SemaphoreType.DMA((15,)), pltpu.SemaphoreType.DMA((15,)), pltpu.SemaphoreType.DMA((2,))]

    def events(self, ins, outs, scratch):
        (own,), (full,) = ins, outs
        hold, ss, rs, local = scratch
        o, half = self.order, self.cols // 2
        _, y, z, c = place()
        f, g = (y, z) if o == 0 else (z, y)

        def block(fk, gk, core):
            return full.at[fk, gk, core] if o == 0 else full.at[gk, fk, core]

        def column(gk, core):
            return full.at[:, gk, core] if o == 0 else full.at[gk, :, core]

        lo, hi = pl.ds(0, half), pl.ds(half, half)
        fp, fm, f2 = step_to(f, 1), step_to(f, -1), step_to(f, 2)
        gp, gm, g2 = step_to(g, 1), step_to(g, -1), step_to(g, 2)
        me = block(f, g, c)

        def cols_of(gk, part):
            return full.at[:, gk, c, :, part] if o == 0 else full.at[gk, :, c, :, part]

        def part_of(fk, part):
            return full.at[fk, g, c, :, part] if o == 0 else full.at[g, fk, c, :, part]

        up1, dn1 = mate(o, 0, 1), mate(o, 0, -1)
        up2, dn2 = mate(o, 1, 1), mate(o, 1, -1)
        p = partner()
        table = [
            (own, me, block(fm, g, c), up1),
            (own, me, block(fp, g, c), dn1),
            (part_of(fm, lo), part_of(fm, lo), part_of(f2, lo), up1),
            (part_of(fp, hi), part_of(fp, hi), part_of(f2, hi), dn1),
            (column(g, c), column(g, c), column(gm, c), up2),
            (column(g, c), column(g, c), column(gp, c), dn2),
            (cols_of(gm, lo), cols_of(gm, lo), cols_of(g2, lo), up2),
            (cols_of(gp, hi), cols_of(gp, hi), cols_of(g2, hi), dn2),
            (own, me, block(f, g, 1 - c), p),
            (block(fm, g, c), block(fm, g, c), block(fm, g, 1 - c), p),
            (block(fp, g, c), block(fp, g, c), block(fp, g, 1 - c), p),
            (block(f2, g, c), block(f2, g, c), block(f2, g, 1 - c), p),
            (column(gm, c), column(gm, c), column(gm, 1 - c), p),
            (column(gp, c), column(gp, c), column(gp, 1 - c), p),
            (column(g2, c), column(g2, c), column(g2, 1 - c), p),
        ]

        def start(*numbers):
            for n in numbers:
                src, dst, _, to = table[n]
                remote(src, dst, ss.at[n], rs.at[n], to).start()

        def arrived(*numbers):
            for n in numbers:
                _, _, here, to = table[n]
                remote(here, here, ss.at[n], rs.at[n], to).wait_recv()

        def e0():
            start(0, 1, 8)
            pltpu.make_async_copy(own, hold, local.at[0]).start()

        def e1():
            pltpu.make_async_copy(own, hold, local.at[0]).wait()
            pltpu.make_async_copy(hold, me, local.at[1]).start()
            arrived(0, 1)
            start(2, 3, 9, 10)

        def e2():
            pltpu.make_async_copy(hold, me, local.at[1]).wait()
            arrived(2, 3)
            start(4, 5, 11)

        def e3():
            arrived(4, 5)
            start(6, 7, 12, 13)

        def e4():
            arrived(6, 7)
            start(14)

        def e5():
            arrived(*range(8, 15))
            for n in range(15):
                src, dst, _, to = table[n]
                remote(src, dst, ss.at[n], rs.at[n], to).wait_send()

        return [e0, e1, e2, e3, e4, e5]


def added(*refs_at):
    total = refs_at[0].astype(F32)
    for r in refs_at[1:]:
        total = total + r.astype(F32)
    return total.astype(BF)


class Ring:
    def __init__(self, slot, n, got, ss, rs, k, up, down):
        self.slot, self.n, self.got, self.ss, self.rs = slot, n, got, ss, rs
        self.k, self.up, self.down = k, up, down

    def copy(self, kind, d):
        k, a = self.k, d
        if kind == TT:
            src = self.slot(a, step_to(k, 2))
        elif kind == UU:
            src = self.slot(1 - a, step_to(k, 1 - 2 * d))
        else:
            src = self.slot(a, step_to(k, 1 - 2 * d))
        return remote(src, self.got.at[kind, d], self.ss.at[kind, d], self.rs.at[kind, d], self.down if d else self.up)

    def first(self):
        for d in (0, 1):
            self.copy(TT, d).start()
        for d in (0, 1):
            self.copy(UU, d).start()

    def second_add(self):
        for d in (0, 1):
            self.copy(TT, d).wait_recv()
        for d in (0, 1):
            ref = self.slot(d, step_to(self.k, 1 - 2 * d))
            for i in range(self.n):
                ref[i] = added(ref[i], self.got[TT, d, i])

    def second_send(self):
        for d in (0, 1):
            self.copy(VV, d).start()

    def last(self, out):
        for kind in (UU, VV):
            for d in (0, 1):
                self.copy(kind, d).wait_recv()
        for a in (0, 1):
            ref = self.slot(a, self.k)
            for i in range(self.n):
                out(a, i, added(ref[i], self.got[VV, a, i], self.got[UU, 1 - a, i]))

    def drain(self):
        for kind in (TT, UU, VV):
            for d in (0, 1):
                self.copy(kind, d).wait_send()


class SumA:
    far = False

    def __init__(self, grad):
        rows, cols = grad.shape
        self.R, self.C = rows // 32, cols // 4
        R, C = self.R, self.C
        self.inputs = [grad.reshape(4, 4, 2, R, cols)]
        self.outs = [jax.ShapeDtypeStruct((2, 2, 4, R, C), BF)]
        self.out_specs = [ANY]
        D = pltpu.SemaphoreType.DMA
        self.scratch = [pltpu.VMEM((4, 4, 4, R, C), BF), pltpu.VMEM((4, 4, 4, R, C), BF), pltpu.VMEM((2, 3, 2, 4, R, C), BF), pltpu.VMEM((2, 2, 4, R, C), BF)]
        self.scratch += [D((4,)), D((4,)), D((4,)), D((2, 3, 2)), D((2, 3, 2)), D]

    def events(self, ins, outs, scratch):
        (g,), (out,) = ins, outs
        H, other, got, F, ls, ds, dr, ss, rs, os = scratch
        C = self.C
        _, y, z, c = place()

        def load(q):
            return pltpu.make_async_copy(g.at[:, :, c, :, pl.ds(q * C, C)], H.at[q], ls.at[q])

        def cross(q):
            return remote(g.at[:, :, 1 - c, :, pl.ds(q * C, C)], other.at[q], ds.at[q], dr.at[q], partner())

        def slot(o):
            return lambda ab, k: H.at[2 * o + ab, k] if o == 0 else H.at[2 * o + ab, :, k]

        rings = [Ring(slot(o), 4, got.at[o], ss.at[o], rs.at[o], (y, z)[o], mate(o, 0, 1), mate(o, 0, -1)) for o in (0, 1)]

        def e0():
            for q in range(4):
                cross(q).start()
                load(q).start()

        def e1():
            for q in range(4):
                load(q).wait()
                cross(q).wait_recv()

                def body(i, _):
                    a, b = i // 4, i % 4
                    H[q, a, b] = added(H[q, a, b], other[q, a, b])
                    return 0

                lax.fori_loop(0, 16, body, 0)

        def e2():
            for r in rings:
                r.first()

        def e3():
            for r in rings:
                r.second_add()

        def e4():
            for r in rings:
                r.second_send()

        def e5():
            for o, r in enumerate(rings):

                def put(a, i, value, o=o):
                    F[o, a, i] = value

                r.last(put)

        def e6():
            pltpu.make_async_copy(F, out, os).start()
            for r in rings:
                r.drain()
            for q in range(4):
                cross(q).wait_send()
            pltpu.make_async_copy(F, out, os).wait()

        return [e0, e1, e2, e3, e4, e5, e6]


class SumB:
    far = True

    def __init__(self, part):
        _, _, _, R, C = part.shape
        self.R, self.C = R, C
        self.inputs = [part]
        self.outs = [jax.ShapeDtypeStruct((R, 4 * C), BF)]
        self.out_specs = [ANY]
        D = pltpu.SemaphoreType.DMA
        self.scratch = [pltpu.VMEM((2, 2, 4, R, C), BF), pltpu.VMEM((2, 3, 2, 1, R, C), BF), pltpu.VMEM((4, 4, R, C), BF), pltpu.VMEM((R, 4 * C), BF)]
        self.scratch += [D, D((2, 3, 2)), D((2, 3, 2)), D((3,)), D((3,)), D]

    def events(self, ins, outs, scratch):
        (part,), (out,) = ins, outs
        F, got, X, done, ls, ss, rs, xs, xr, os = scratch
        C = self.C
        x, y, z, c = place()

        def slot(o):
            return lambda ab, k: F.at[o, ab, pl.ds(k, 1)]

        rings = [Ring(slot(o), 1, got.at[o], ss.at[o], rs.at[o], (z, y)[o], mate(o, 1, 1), mate(o, 1, -1)) for o in (0, 1)]

        def over(d):
            return remote(X.at[x], X.at[x], xs.at[d - 1], xr.at[d - 1], {"r": step_to(x, d)})

        def came(d):
            src = X.at[step_to(x, -d)]
            return remote(src, src, xs.at[d - 1], xr.at[d - 1], {"r": step_to(x, d)})

        def e0():
            pltpu.make_async_copy(part, F, ls).start()
            pltpu.make_async_copy(part, F, ls).wait()
            for r in rings:
                r.first()

        def e1():
            for r in rings:
                r.second_add()

        def e2():
            for r in rings:
                r.second_send()

        def e3():
            for o, r in enumerate(rings):

                def put(a, i, value, o=o):
                    X[x, 2 * o + a] = value

                r.last(put)

        def e4():
            for d in (1, 3, 2):
                over(d).start()

        def e5():
            for d in (1, 3, 2):
                came(d).wait_recv()
            for q in range(4):
                done[:, q * C : (q + 1) * C] = added(*(X[i, q] for i in range(4)))

        def e6():
            pltpu.make_async_copy(done, out, os).start()
            for r in rings:
                r.drain()
            for d in (1, 3, 2):
                over(d).wait_send()
            pltpu.make_async_copy(done, out, os).wait()

        return [e0, e1, e2, e3, e4, e5, e6]


def run(name, number, steps, arrays, specs, outs, out_specs, compute, jobs=(), when=None, flops=0):
    n_in, n_out = len(arrays), len(outs)
    job_in = [a for j in jobs for a in j.inputs]
    job_out = [a for j in jobs for a in j.outs]

    def body(*refs):
        ins, rest = refs[:n_in], refs[n_in:]
        jin, rest = rest[: len(job_in)], rest[len(job_in) :]
        mouts, rest = rest[:n_out], rest[n_out:]
        jout, scratch = rest[: len(job_out)], rest[len(job_out) :]
        t = pl.program_id(0)
        lists = []
        for j in jobs:
            a, jin = jin[: len(j.inputs)], jin[len(j.inputs) :]
            b, jout = jout[: len(j.outs)], jout[len(j.outs) :]
            c, scratch = scratch[: len(j.scratch)], scratch[len(j.scratch) :]
            lists.append(j.events(a, b, c))
        if jobs:

            @pl.when(t == 0)
            def _():
                barrier = pltpu.get_barrier_semaphore()
                them = [mate(0, w, d) for w in (0, 1) for d in (1, -1)] + [partner()]
                if any(j.far for j in jobs):
                    x = lax.axis_index("r")
                    them += [{"r": step_to(x, d)} for d in (1, 2, 3)]
                for device in them:
                    pl.semaphore_signal(barrier, inc=1, device_id=device, device_id_type=MESH)
                pl.semaphore_wait(barrier, len(them))

        table = {}
        for j, events in enumerate(lists):
            for i, e in enumerate(events):
                at = when[j][i] if when and i < len(when[j]) else steps
                table.setdefault(min(at, steps), []).append((i, j, e))
        for at in sorted(table):
            if at < steps:

                @pl.when(t == at)
                def _(at=at):
                    for _, _, e in sorted(table[at], key=lambda v: v[:2]):
                        e()

        if compute is not None:
            compute(t, ins, mouts)
        if steps in table:

            @pl.when(t == steps - 1)
            def _():
                for _, _, e in sorted(table[steps], key=lambda v: v[:2]):
                    e()

    got = pl.pallas_call(
        body,
        name=name,
        grid=(steps,),
        out_shape=list(outs) + job_out,
        in_specs=list(specs) + [ANY] * len(job_in),
        out_specs=list(out_specs) + [s for j in jobs for s in j.out_specs],
        scratch_shapes=[s for j in jobs for s in j.scratch],
        compiler_params=pltpu.CompilerParams(
            dimension_semantics=("arbitrary",),
            vmem_limit_bytes=66_000_000,
            **(dict(collective_id=number, has_side_effects=True) if jobs else {}),
        ),
        cost_estimate=pl.CostEstimate(flops=flops, bytes_accessed=50_000_000, transcendentals=0),
    )(*arrays, *job_in)
    return list(got)


def fixed(shape):
    return pl.BlockSpec(shape, lambda t: (0,) * len(shape), pipeline_mode=pl.Buffered(1))


def across(rows, cols):
    return pl.BlockSpec((rows, cols), lambda t: (0, t))


def down_by(rows, cols):
    return pl.BlockSpec((rows, cols), lambda t: (t, 0))


def nn(a, b):
    return jnp.dot(a, b, preferred_element_type=F32)


def nt(a, b):
    return lax.dot_general(a, b, (((1,), (1,)), ((), ())), preferred_element_type=F32)


def tn(a, b):
    return lax.dot_general(a, b, (((0,), (0,)), ((), ())), preferred_element_type=F32)


def shape(*dims, dtype=BF):
    return jax.ShapeDtypeStruct(dims, dtype)


ROWS = 512


def by_rows(total, fn):
    def body(i, _):
        fn(pl.ds(pl.multiple_of(i * ROWS, ROWS), ROWS))
        return 0

    lax.fori_loop(0, total // ROWS, body, 0)


def glu(t, ins, outs):
    a, wg, wu = ins
    gate_ref, up_ref, hid_ref = outs

    def part(rows):
        gate, up = nn(a[rows, :], wg[...]), nn(a[rows, :], wu[...])
        gate_ref[rows, :] = gate
        up_ref[rows, :] = up
        hid_ref[rows, :] = (gate * jax.nn.sigmoid(gate) * up).astype(BF)

    by_rows(a.shape[0], part)


def glu_back(by_hid, gate, up):
    by_hid = by_hid.astype(BF).astype(F32)
    sig = jax.nn.sigmoid(gate)
    act = gate * sig
    return (act * up).astype(BF), (by_hid * up * (sig + act * (1.0 - sig))).astype(BF), (by_hid * act).astype(BF)


def both_ways(t, ins, outs):
    a, dy, wg, wu, wd = ins
    hid_ref, dg_ref, du_ref = outs

    def part(rows):
        gate, up = nn(a[rows, :], wg[...]), nn(a[rows, :], wu[...])
        hid_ref[rows, :], dg_ref[rows, :], du_ref[rows, :] = glu_back(nt(dy[rows, :], wd[...]), gate, up)

    by_rows(a.shape[0], part)


def back(t, ins, outs):
    dy, wd, gate, up = ins
    dg_ref, du_ref = outs

    def part(rows):
        _, dg_ref[rows, :], du_ref[rows, :] = glu_back(nt(dy[rows, :], wd[...]), gate[rows, :], up[rows, :])

    by_rows(dy.shape[0], part)


def lower(t, ins, outs):
    hid, wd, h = ins
    outs[0][...] = h[...] + nn(hid[...], wd[...]).astype(BF)


def grad_two(t, ins, outs):
    at, dg, du = ins
    outs[0][...] = nn(at[...], dg[...]).astype(BF)
    outs[1][...] = nn(at[...], du[...]).astype(BF)


def grad_down(t, ins, outs):
    hid, dy = ins
    outs[0][...] = tn(hid[...], dy[...]).astype(BF)


def grad_a(t, ins, outs):
    dg, du, wg, wu = ins
    outs[0][...] = nt(dg[...], wg[...]).astype(BF) + nt(du[...], wu[...]).astype(BF)


def normed(h):
    wide = h.astype(F32)
    scale = lax.rsqrt(jnp.mean(wide**2, -1, keepdims=True) + 1e-6)
    return (wide * scale).astype(BF)


def adamw(w, m, v, g):
    m = 0.9 * m + 0.1 * g
    v = 0.95 * v + 0.05 * g * g
    step = m * lax.rsqrt(v + 1e-8) + 0.1 * w
    return (w - 0.02 * step).astype(BF), m, v


def solution(mesh):
    def step(x, dy, *arrays):
        (wg, wu, wd), m, v = (arrays[i : i + 3] for i in (0, 3, 6))
        x, dy = x[0], dy[0]
        N, D = x.shape
        FF = wg.shape[2]
        B, TB = 256, 256
        T, TN = FF // B, N // TB
        one = 2 * N * D * FF
        flat = lambda w: w.reshape(-1, w.shape[-1])
        tok, wide, ffd = (N, D), shape(N, FF), shape(FF, D)

        wg1, wu1 = map(flat, run("fetch_0", 1, 1, [], [], [], [], None, [Gather(0, wg[0]), Gather(1, wu[0])], flops=one))
        a1 = normed(x)
        gate1, up1, hid1, wd1, wg2 = run(
            "glu_0", 2, T, [a1, wg1, wu1], [fixed(tok), across(D, B), across(D, B)],
            [shape(N, FF, dtype=F32), shape(N, FF, dtype=F32), wide], [across(N, B)] * 3, glu,
            [Gather(0, wd[0]), Gather(1, wg[1])], [[0, 2, 4, 8, 12], [0, 2, 4, 8, 12]], 2 * one,
        )
        wd1, wg2 = flat(wd1), flat(wg2)
        h1, wu2, wd2 = run(
            "lower_0", 3, TN, [hid1, wd1, x], [down_by(TB, FF), fixed((FF, D)), down_by(TB, D)],
            [shape(N, D)], [down_by(TB, D)], lower,
            [Gather(0, wu[1]), Gather(1, wd[1])], [[0, 2, 4], [0, 2, 4]], one,
        )
        wu2, wd2 = flat(wu2), flat(wd2)
        a2, back_norm = jax.vjp(normed, h1)
        hid2, dg2, du2 = run(
            "both_1", 0, T, [a2, dy, wg2, wu2, wd2], [fixed(tok), fixed(tok), across(D, B), across(D, B), down_by(B, D)],
            [wide] * 3, [across(N, B)] * 3, both_ways, flops=3 * one,
        )
        (gd2,) = run("grad_down_1", 0, T, [hid2, dy], [across(N, B), fixed(tok)], [ffd], [down_by(B, D)], grad_down, flops=one)
        gg2, gu2, fd2 = run(
            "grad_two_1", 4, T, [a2.T, dg2, du2], [fixed((D, N)), across(N, B), across(N, B)],
            [shape(D, FF)] * 2, [across(D, B)] * 2, grad_two, [SumA(gd2)], [[0, 3, 4, 9, 10]], 2 * one,
        )
        by_a, fg2, sd2 = run(
            "grad_a_1", 5, TN, [dg2, du2, wg2, wu2], [down_by(TB, FF)] * 2 + [fixed((D, FF))] * 2,
            [shape(N, D)], [down_by(TB, D)], grad_a, [SumA(gg2), SumB(fd2)], [[0, 2, 3, 6, 7], [0, 1, 2, 3, 4, 7]], 2 * one,
        )
        dh = dy + back_norm(by_a)[0]
        dg1, du1, fu2, sg2 = run(
            "back_0", 6, T, [dh, wd1, gate1, up1], [fixed(tok), down_by(B, D), across(N, B), across(N, B)],
            [wide] * 2, [across(N, B)] * 2, back, [SumA(gu2), SumB(fg2)], [[0, 3, 4, 9, 10], [0, 2, 3, 5, 6, 13]], one,
        )
        gd1, su2 = run(
            "grad_down_0", 7, T, [hid1, dh], [across(N, B), fixed(tok)], [ffd], [down_by(B, D)], grad_down,
            [SumB(fu2)], [[0, 3, 4, 6, 7, 13]], one,
        )
        gg1, gu1, fd1 = run(
            "grad_two_0", 8, T, [a1.T, dg1, du1], [fixed((D, N)), across(N, B), across(N, B)],
            [shape(D, FF)] * 2, [across(D, B)] * 2, grad_two, [SumA(gd1)], [[0, 3, 4, 9, 10]], 2 * one,
        )
        fg1, fu1, sd1 = run("sum_a", 9, 1, [], [], [], [], None, [SumA(gg1), SumA(gu1), SumB(fd1)], flops=one)
        sg1, su1 = run("sum_b", 10, 1, [], [], [], [], None, [SumB(fg1), SumB(fu1)], flops=one)

        sums = [(sg1, sg2), (su1, su2), (sd1, sd2)]
        gradients = [jnp.stack(pair).astype(F32) for pair in sums]
        new = [adamw(w.astype(F32), mm, vv, g) for w, mm, vv, g in zip((wg, wu, wd), m, v, gradients, strict=True)]
        return tuple(one_[which] for which in range(3) for one_ in new)

    states, cut = P(("rep", "r", "s"), None, None), P(None, "s", None)
    return jax.shard_map(
        step,
        mesh=mesh,
        in_specs=(states, states) + (cut,) * 9,
        out_specs=(P("rep", "s", None),) * 9,
        check_vma=False,
    )
```

time: 1060 us -> 630 us (0.59)
  waiting for transfers between devices: 607 us -> 0 us
  Pallas kernels: 0 us -> 557 us
  matrix products: 396 us -> 0 us
  other arithmetic: 15.8 us -> 45.6 us
  between operations: 14.2 us -> 0.88 us
    pallas_call x0 -> x12, Pallas kernels: none -> 557 us  [run(): pl.pallas_call(body, name=name, grid=(steps,), out_shape=list(outs) + job...]
    dot_general x15 -> x0, matrix products: 396 us -> none  [the longest x5 146 us: layer(): gate = jnp.dot(a, w['w_gate'], preferred_element_type=jnp.float32)]
    reduce_scatter x6 -> x0, waiting for transfers between devices: 385 us -> none  [summed(): lax.psum_scatter(term, 's', scatter_dimension=0, tiled=True)]
    all_gather x6 -> x0, waiting for transfers between devices: 168 us -> none  [fetched(): lax.all_gather(w[number], 's', axis=0, tiled=True)]
    psum x1 -> x0, waiting for transfers between devices: 51.6 us -> none  [summed(): lax.psum(lax.psum_scatter(term, 's', scatter_dimension=0, tiled=True), 'r')]
    convert_element_type x2 -> x5, other arithmetic: 7.86 us -> 19 us  [the longest x2 10.6 us: normed(): return (wide * scale).astype(BF)]
  transfers between devices with their start and end apart: 13 -> 0, of which waited for: 12 -> 0; matrix products, arithmetic and copies ran while one was open for 29% -> 0% of each run, Pallas kernels for 0% -> 0%
where the time goes in v1:
time: 630 us; the launch traced here: 626 us
  Pallas kernels  557 us (88%)
  other arithmetic  45.6 us (7%)
  local copies, waits for them, and re-layouts  23 us (4%)
    pallas_call x12, Pallas kernels, run(): pl.pallas_call(body, name=name, grid=(steps,), out_shape=list(outs) + job...  557 us

profile of v1, /device:TPU:1, one launch (start us, length us, event | category | flops | bytes accessed | tf_op | source)
XLA Modules:
  0.0 626.4 jit_solution(18027076929708775852)
XLA Ops:
  0.6 6.5 %copy.20 = bf16[1,2048,1024]{1,2,0:T(8,128)(2,1)} copy(bf16[1,2048,1024]{2,1,0:T(8,128)(2,1)} %param.11) | data formatting | bytes 8388608 | tf_op args[0]
  10.9 5.7 fusion.1
  16.5 6.4 %copy.21.refs_0_ = bf16[2048,1024]{1,0:T(8,128)(2,1)} copy(bf16[2048,1024]{0,1:T(8,128)(2,1)} %fusion.1) | data formatting | bytes 8388608 | tf_op jit(solution)/shard_map/convert_element_type | solution.py:525
  23.9 52.2 %fetch_0.1 = (bf16[4,4,2,32,3584]{4,3,2,1,0:T(8,128)(2,1)}, bf16[4,4,2,32,3584]{4,3,2,1,0:T(8,128)(2,1)}) custom-call(bf16[32,3584]{1,0:T(8,128)(2,1)} %get-tuple-element.90.refs_0_, bf16[32,3584]{1,0:T(8,128)(2,1)} %get-tuple-element.87.refs_1_), custom_call_target="tpu_custom_call" | custom-call | flops 15032385536 | bytes 50000000 | tf_op jit(solution)/shard_map/fetch_0/pallas_call | solution.py:403
  76.9 59.8 %glu_0.1 = (f32[2048,3584]{1,0:T(8,128)}, f32[2048,3584]{1,0:T(8,128)}, bf16[2048,3584]{1,0:T(8,128)(2,1)}, bf16[4,4,2,112,1024]{4,3,2,1,0:T(8,128)(2,1)}, bf16[4,4,2,32,3584]{4,3,2,1,0:T(8,128)(2,1)}) custom-call(bf16[2048,1024]{1,0:T(8,128)(2,1)} %copy.21.refs_0_, bf16[1024,3584]{1,0:T(8,128)(2,1)} %bitcast.58, bf16[1024,3584]{1,0:T(8,128)(2,1)} %bitcast.59, ...), custom_call_target="tpu_custom_call" | custom-call | flops 30064771072 | bytes 50000000 | tf_op jit(solution)/shard_map/glu_0/pallas_call | solution.py:403
  136.7 52.7 %lower_0.1 = (bf16[2048,1024]{1,0:T(8,128)(2,1)}, bf16[4,4,2,32,3584]{4,3,2,1,0:T(8,128)(2,1)}, bf16[4,4,2,112,1024]{4,3,2,1,0:T(8,128)(2,1)}) custom-call(bf16[2048,3584]{1,0:T(8,128)(2,1)} %get-tuple-element.44.refs_0_, bf16[3584,1024]{1,0:T(8,128)(2,1)} %bitcast.42, bf16[2048,1024]{1,0:T(8,128)(2,1)} %bitcast.47, ...), custom_call_target="tpu_custom_call" | custom-call | flops 15032385536 | bytes 50000000 | tf_op jit(solution)/shard_map/lower_0/pallas_call | solution.py:403
  189.5 3.1 fusion.4
  192.6 4.9 fusion.5.refs_0_
  197.5 63.4 %both_1.1 = (bf16[2048,3584]{1,0:T(8,128)(2,1)}, bf16[2048,3584]{1,0:T(8,128)(2,1)}, bf16[2048,3584]{1,0:T(8,128)(2,1)}) custom-call(bf16[2048,1024]{1,0:T(8,128)(2,1)} %fusion.5.refs_0_, bf16[2048,1024]{1,0:T(8,128)(2,1)} %bitcast.45, bf16[1024,3584]{1,0:T(8,128)(2,1)} %bitcast.54, bf16[1024,3584]{1,0:T(8,128)(2,1)} %bitcast.56, bf16[3584,1024]{1,0:T(8,128)(2,1)} %bitcast.61), custom_call_target="tpu_custom_call" | custom-call | flops 45097156608 | bytes 50000000 | tf_op jit(solution)/shard_map/both_1/pallas_call | solution.py:403
  260.9 5.0 fusion.31
  265.8 6.5 %copy.23.refs_0_ = bf16[1024,2048]{1,0:T(8,128)(2,1)} copy(bf16[1024,2048]{0,1:T(8,128)(2,1)} %fusion.31) | data formatting | bytes 8388608 | tf_op jit(solution)/shard_map/transpose | solution.py:568
  272.4 22.3 %grad_down_1.1 = bf16[3584,1024]{1,0:T(8,128)(2,1)} custom-call(bf16[2048,3584]{1,0:T(8,128)(2,1)} %get-tuple-element.52.refs_0_, bf16[2048,1024]{1,0:T(8,128)(2,1)} %bitcast.46), custom_call_target="tpu_custom_call" | custom-call | flops 15032385536 | bytes 50000000 | tf_op jit(solution)/shard_map/grad_down_1/pallas_call | solution.py:403
  294.6 43.6 %grad_two_1.1 = (bf16[1024,3584]{1,0:T(8,128)(2,1)}, bf16[1024,3584]{1,0:T(8,128)(2,1)}, bf16[2,2,4,112,256]{4,3,2,1,0:T(8,128)(2,1)}) custom-call(bf16[1024,2048]{1,0:T(8,128)(2,1)} %copy.23.refs_0_, bf16[2048,3584]{1,0:T(8,128)(2,1)} %get-tuple-element.50.refs_1_.refs_0_, bf16[2048,3584]{1,0:T(8,128)(2,1)} %get-tuple-element.51.refs_2_.refs_1_, ...), custom_call_target="tpu_custom_call" | custom-call | flops 30064771072 | bytes 50000000 | tf_op jit(solution)/shard_map/grad_two_1/pallas_call | solution.py:403
  338.3 50.9 %grad_a_1.1 = (bf16[2048,1024]{1,0:T(8,128)(2,1)}, bf16[2,2,4,32,896]{4,3,2,1,0:T(8,128)(2,1)}, bf16[112,1024]{1,0:T(8,128)(2,1)}) custom-call(bf16[2048,3584]{1,0:T(8,128)(2,1)} %get-tuple-element.50.refs_1_.refs_0_, bf16[2048,3584]{1,0:T(8,128)(2,1)} %get-tuple-element.51.refs_2_.refs_1_, bf16[1024,3584]{1,0:T(8,128)(2,1)} %bitcast.55, ...), custom_call_target="tpu_custom_call" | custom-call | flops 30064771072 | bytes 50000000 | tf_op jit(solution)/shard_map/grad_a_1/pallas_call | solution.py:403
  389.2 4.8 fusion.6
  395.1 5.2 fusion.7.refs_0_.refs_1_
  400.3 52.8 %back_0.1 = (bf16[2048,3584]{1,0:T(8,128)(2,1)}, bf16[2048,3584]{1,0:T(8,128)(2,1)}, bf16[2,2,4,32,896]{4,3,2,1,0:T(8,128)(2,1)}, bf16[32,3584]{1,0:T(8,128)(2,1)}) custom-call(bf16[2048,1024]{1,0:T(8,128)(2,1)} %fusion.7.refs_0_.refs_1_, bf16[3584,1024]{1,0:T(8,128)(2,1)} %bitcast.43, f32[2048,3584]{1,0:T(8,128)} %get-tuple-element.56.refs_2_, ...), custom_call_target="tpu_custom_call" | custom-call | flops 15032385536 | bytes 50000000 | tf_op jit(solution)/shard_map/back_0/pallas_call | solution.py:403
  453.1 5.5 fusion.30.refs_0_
  458.6 28.5 %grad_down_0.1 = (bf16[3584,1024]{1,0:T(8,128)(2,1)}, bf16[32,3584]{1,0:T(8,128)(2,1)}) custom-call(bf16[2048,3584]{1,0:T(8,128)(2,1)} %get-tuple-element.44.refs_0_, bf16[2048,1024]{1,0:T(8,128)(2,1)} %fusion.7.refs_0_.refs_1_, bf16[2,2,4,32,896]{4,3,2,1,0:T(8,128)(2,1)} %get-tuple-element.62.refs_2_), custom_call_target="tpu_custom_call" | custom-call | flops 15032385536 | bytes 50000000 | tf_op jit(solution)/shard_map/grad_down_0/pallas_call | solution.py:403
  487.1 44.5 %grad_two_0.1 = (bf16[1024,3584]{1,0:T(8,128)(2,1)}, bf16[1024,3584]{1,0:T(8,128)(2,1)}, bf16[2,2,4,112,256]{4,3,2,1,0:T(8,128)(2,1)}) custom-call(bf16[1024,2048]{1,0:T(8,128)(2,1)} %fusion.30.refs_0_, bf16[2048,3584]{1,0:T(8,128)(2,1)} %get-tuple-element.60.refs_1_, bf16[2048,3584]{1,0:T(8,128)(2,1)} %get-tuple-element.61.refs_2_, ...), custom_call_target="tpu_custom_call" | custom-call | flops 30064771072 | bytes 50000000 | tf_op jit(solution)/shard_map/grad_two_0/pallas_call | solution.py:403
  531.6 52.9 %sum_a.1 = (bf16[2,2,4,32,896]{4,3,2,1,0:T(8,128)(2,1)}, bf16[2,2,4,32,896]{4,3,2,1,0:T(8,128)(2,1)}, bf16[112,1024]{1,0:T(8,128)(2,1)}) custom-call(bf16[4,4,2,32,3584]{4,3,2,1,0:T(8,128)(2,1)} %bitcast.63, bf16[4,4,2,32,3584]{4,3,2,1,0:T(8,128)(2,1)} %bitcast.64, bf16[2,2,4,112,256]{4,3,2,1,0:T(8,128)(2,1)} %get-tuple-element.66.refs_2_), custom_call_target="tpu_custom_call" | custom-call | flops 15032385536 | bytes 50000000 | tf_op jit(solution)/shard_map/sum_a/pallas_call | solution.py:403
  584.5 33.3 %sum_b.1 = (bf16[32,3584]{1,0:T(8,128)(2,1)}, bf16[32,3584]{1,0:T(8,128)(2,1)}) custom-call(bf16[2,2,4,32,896]{4,3,2,1,0:T(8,128)(2,1)} %get-tuple-element.67.refs_0_, bf16[2,2,4,32,896]{4,3,2,1,0:T(8,128)(2,1)} %get-tuple-element.68.refs_1_), custom_call_target="tpu_custom_call" | custom-call | flops 15032385536 | bytes 50000000 | tf_op jit(solution)/shard_map/sum_b/pallas_call | solution.py:403
  617.9 3.4 fusion.10
  621.4 3.3 fusion.14
  (35 shorter events, 8.3 us)
Async XLA Ops:
  10.3 0.6 copy-start.12
  10.9 12.1 %copy-start.2 = (bf16[2,32,3584]{2,1,0:T(8,128)(2,1)S(1)}, bf16[2,32,3584]{2,1,0:T(8,128)(2,1)}, u32[]{:S(2)}) copy-start(bf16[2,32,3584]{2,1,0:T(8,128)(2,1)} %param.13) | copy-start | bytes 1376260
  10.9 12.1 %copy-start.4 = (bf16[2,32,3584]{2,1,0:T(8,128)(2,1)S(1)}, bf16[2,32,3584]{2,1,0:T(8,128)(2,1)}, u32[]{:S(2)}) copy-start(bf16[2,32,3584]{2,1,0:T(8,128)(2,1)} %param.14) | copy-start | bytes 1376260
  23.9 52.3 %copy-start.6 = (bf16[2,112,1024]{2,1,0:T(8,128)(2,1)S(1)}, bf16[2,112,1024]{2,1,0:T(8,128)(2,1)}, u32[]{:S(2)}) copy-start(bf16[2,112,1024]{2,1,0:T(8,128)(2,1)} %param.15) | copy-start | bytes 1376260
  389.2 4.8 copy-start
  389.2 5.9 copy-start.1
  400.3 52.8 %copy-start.13 = (f32[2048]{0:T(1024)S(1)}, f32[2048]{0:T(1024)}, u32[]{:S(2)}) copy-start(f32[2048]{0:T(1024)} %copy-done.12) | copy-start | bytes 24580
  584.5 33.4 %copy-start.3 = (bf16[2,32,3584]{2,1,0:T(8,128)(2,1)S(1)}, bf16[2,32,3584]{2,1,0:T(8,128)(2,1)}, u32[]{:S(2)}) copy-start(bf16[2,32,3584]{2,1,0:T(8,128)(2,1)} %param.13) | copy-start | bytes 1376260
  584.5 36.8 %copy-start.5 = (bf16[2,32,3584]{2,1,0:T(8,128)(2,1)S(1)}, bf16[2,32,3584]{2,1,0:T(8,128)(2,1)}, u32[]{:S(2)}) copy-start(bf16[2,32,3584]{2,1,0:T(8,128)(2,1)} %param.14) | copy-start | bytes 1376260
  617.9 6.8 %copy-start.7 = (bf16[2,112,1024]{2,1,0:T(8,128)(2,1)S(1)}, bf16[2,112,1024]{2,1,0:T(8,128)(2,1)}, u32[]{:S(2)}) copy-start(bf16[2,112,1024]{2,1,0:T(8,128)(2,1)} %param.15) | copy-start | bytes 1376260
  617.9 6.8 %copy-start.8 = (f32[2,112,1024]{2,1,0:T(8,128)S(1)}, f32[2,112,1024]{2,1,0:T(8,128)}, u32[]{:S(2)}) copy-start(f32[2,112,1024]{2,1,0:T(8,128)} %param.21) | copy-start | bytes 2752516
  617.9 6.8 %copy-start.9 = (f32[2,112,1024]{2,1,0:T(8,128)S(1)}, f32[2,112,1024]{2,1,0:T(8,128)}, u32[]{:S(2)}) copy-start(f32[2,112,1024]{2,1,0:T(8,128)} %param.18) | copy-start | bytes 2752516
  617.9 6.8 %copy-start.10 = (bf16[112,1024]{1,0:T(8,128)(2,1)S(1)}, bf16[112,1024]{1,0:T(8,128)(2,1)}, u32[]{:S(2)}) copy-start(bf16[112,1024]{1,0:T(8,128)(2,1)} %get-tuple-element.74) | copy-start | bytes 688132
  617.9 6.8 %copy-start.11 = (bf16[112,1024]{1,0:T(8,128)(2,1)S(1)}, bf16[112,1024]{1,0:T(8,128)(2,1)}, u32[]{:S(2)}) copy-start(bf16[112,1024]{1,0:T(8,128)(2,1)} %get-tuple-element.73) | copy-start | bytes 688132

commit v2 on v1

--- a/solution.py
+++ b/solution.py
@@ -51,7 +51,7 @@
         self.inputs = [shard]
         self.outs = [jax.ShapeDtypeStruct((4, 4, 2, rows, cols), BF)]
         self.out_specs = [ANY]
-        self.scratch = [pltpu.VMEM((rows, cols), BF), pltpu.SemaphoreType.DMA((15,)), pltpu.SemaphoreType.DMA((15,)), pltpu.SemaphoreType.DMA((2,))]
+        self.scratch = [pltpu.VMEM((rows, cols), BF), pltpu.SemaphoreType.DMA((27,)), pltpu.SemaphoreType.DMA((27,)), pltpu.SemaphoreType.DMA((2,))]
 
     def events(self, ins, outs, scratch):
         (own,), (full,) = ins, outs
@@ -71,32 +71,34 @@
         gp, gm, g2 = step_to(g, 1), step_to(g, -1), step_to(g, 2)
         me = block(f, g, c)
 
-        def cols_of(gk, part):
-            return full.at[:, gk, c, :, part] if o == 0 else full.at[gk, :, c, :, part]
-
-        def part_of(fk, part):
-            return full.at[fk, g, c, :, part] if o == 0 else full.at[g, fk, c, :, part]
-
         up1, dn1 = mate(o, 0, 1), mate(o, 0, -1)
         up2, dn2 = mate(o, 1, 1), mate(o, 1, -1)
         p = partner()
+
+        def half_of(fk, gk, part):
+            return full.at[fk, gk, c, :, part] if o == 0 else full.at[gk, fk, c, :, part]
+
+        line = (f, fm, fp, f2)
         table = [
             (own, me, block(fm, g, c), up1),
             (own, me, block(fp, g, c), dn1),
-            (part_of(fm, lo), part_of(fm, lo), part_of(f2, lo), up1),
-            (part_of(fp, hi), part_of(fp, hi), part_of(f2, hi), dn1),
-            (column(g, c), column(g, c), column(gm, c), up2),
-            (column(g, c), column(g, c), column(gp, c), dn2),
-            (cols_of(gm, lo), cols_of(gm, lo), cols_of(g2, lo), up2),
-            (cols_of(gp, hi), cols_of(gp, hi), cols_of(g2, hi), dn2),
-            (own, me, block(f, g, 1 - c), p),
-            (block(fm, g, c), block(fm, g, c), block(fm, g, 1 - c), p),
-            (block(fp, g, c), block(fp, g, c), block(fp, g, 1 - c), p),
-            (block(f2, g, c), block(f2, g, c), block(f2, g, 1 - c), p),
-            (column(gm, c), column(gm, c), column(gm, 1 - c), p),
-            (column(gp, c), column(gp, c), column(gp, 1 - c), p),
-            (column(g2, c), column(g2, c), column(g2, 1 - c), p),
+            (own, me, block(f, gm, c), up2),
+            (own, me, block(f, gp, c), dn2),
+            (half_of(fm, g, lo), half_of(fm, g, lo), half_of(f2, g, lo), up1),
+            (half_of(fp, g, hi), half_of(fp, g, hi), half_of(f2, g, hi), dn1),
         ]
+        for k in line[1:]:
+            table.append((block(k, g, c), block(k, g, c), block(k, gm, c), up2))
+            table.append((block(k, g, c), block(k, g, c), block(k, gp, c), dn2))
+        for k in line:
+            table.append((half_of(k, gm, lo), half_of(k, gm, lo), half_of(k, g2, lo), up2))
+        for k in line:
+            table.append((half_of(k, gp, hi), half_of(k, gp, hi), half_of(k, g2, hi), dn2))
+        table.append((own, me, block(f, g, 1 - c), p))
+        for k in line[1:]:
+            table.append((block(k, g, c), block(k, g, c), block(k, g, 1 - c), p))
+        for k in (gm, gp, g2):
+            table.append((column(k, c), column(k, c), column(k, 1 - c), p))
 
         def start(*numbers):
             for n in numbers:
@@ -109,35 +111,43 @@
                 remote(here, here, ss.at[n], rs.at[n], to).wait_recv()
 
         def e0():
-            start(0, 1, 8)
+            start(0, 1, 2, 3, 20)
             pltpu.make_async_copy(own, hold, local.at[0]).start()
 
         def e1():
             pltpu.make_async_copy(own, hold, local.at[0]).wait()
             pltpu.make_async_copy(hold, me, local.at[1]).start()
             arrived(0, 1)
-            start(2, 3, 9, 10)
+            start(4, 5, 6, 7, 8, 9, 21, 22)
 
         def e2():
-            pltpu.make_async_copy(hold, me, local.at[1]).wait()
             arrived(2, 3)
-            start(4, 5, 11)
+            start(12, 16)
 
         def e3():
             arrived(4, 5)
-            start(6, 7, 12, 13)
+            start(10, 11, 23)
 
         def e4():
-            arrived(6, 7)
-            start(14)
+            arrived(6, 7, 8, 9)
+            start(13, 17, 14, 18)
 
         def e5():
-            arrived(*range(8, 15))
-            for n in range(15):
+            arrived(10, 11)
+            start(15, 19, 24, 25)
+
+        def e6():
+            arrived(*range(12, 20))
+            start(26)
+
+        def e7():
+            pltpu.make_async_copy(hold, me, local.at[1]).wait()
+            arrived(*range(20, 27))
+            for n in range(27):
                 src, dst, _, to = table[n]
                 remote(src, dst, ss.at[n], rs.at[n], to).wait_send()
 
-        return [e0, e1, e2, e3, e4, e5]
+        return [e0, e1, e2, e3, e4, e5, e6, e7]
 
 
 def added(*refs_at):
@@ -236,12 +246,12 @@
                 load(q).wait()
                 cross(q).wait_recv()
 
-                def body(i, _):
-                    a, b = i // 4, i % 4
-                    H[q, a, b] = added(H[q, a, b], other[q, a, b])
+                def body(a, _):
+                    for b in range(4):
+                        H[q, a, b] = added(H[q, a, b], other[q, a, b])
                     return 0
 
-                lax.fori_loop(0, 16, body, 0)
+                lax.fori_loop(0, 4, body, 0)
 
         def e2():
             for r in rings:
@@ -264,12 +274,14 @@
                 r.last(put)
 
         def e6():
-            pltpu.make_async_copy(F, out, os).start()
+            if out is not None:
+                pltpu.make_async_copy(F, out, os).start()
             for r in rings:
                 r.drain()
             for q in range(4):
                 cross(q).wait_send()
-            pltpu.make_async_copy(F, out, os).wait()
+            if out is not None:
+                pltpu.make_async_copy(F, out, os).wait()
 
         return [e0, e1, e2, e3, e4, e5, e6]
 
@@ -277,19 +289,20 @@
 class SumB:
     far = True
 
-    def __init__(self, part):
-        _, _, _, R, C = part.shape
+    def __init__(self, part, dims=None):
+        R, C = dims or part.shape[3:]
         self.R, self.C = R, C
         self.inputs = [part]
         self.outs = [jax.ShapeDtypeStruct((R, 4 * C), BF)]
         self.out_specs = [ANY]
         D = pltpu.SemaphoreType.DMA
-        self.scratch = [pltpu.VMEM((2, 2, 4, R, C), BF), pltpu.VMEM((2, 3, 2, 1, R, C), BF), pltpu.VMEM((4, 4, R, C), BF), pltpu.VMEM((R, 4 * C), BF)]
-        self.scratch += [D, D((2, 3, 2)), D((2, 3, 2)), D((3,)), D((3,)), D]
-
-    def events(self, ins, outs, scratch):
+        self.scratch = [pltpu.VMEM((2, 2, 4, R, C), BF), pltpu.VMEM((2, 3, 2, 1, R, C), BF), pltpu.VMEM((4, R, C), BF), pltpu.VMEM((4, R, C), BF), pltpu.VMEM((4, R, C), BF)]
+        self.scratch += [D, D((2, 3, 2)), D((2, 3, 2)), D((2, 3)), D((2, 3)), D((4,))]
+
+    def events(self, ins, outs, scratch, held=None):
         (part,), (out,) = ins, outs
-        F, got, X, done, ls, ss, rs, xs, xr, os = scratch
+        F, got, E, X, G, ls, ss, rs, xs, xr, os = scratch
+        F = F if held is None else held
         C = self.C
         x, y, z, c = place()
 
@@ -299,15 +312,26 @@
         rings = [Ring(slot(o), 1, got.at[o], ss.at[o], rs.at[o], (z, y)[o], mate(o, 1, 1), mate(o, 1, -1)) for o in (0, 1)]
 
         def over(d):
-            return remote(X.at[x], X.at[x], xs.at[d - 1], xr.at[d - 1], {"r": step_to(x, d)})
-
-        def came(d):
-            src = X.at[step_to(x, -d)]
-            return remote(src, src, xs.at[d - 1], xr.at[d - 1], {"r": step_to(x, d)})
+            return remote(E.at[step_to(x, d)], X.at[x], xs.at[0, d - 1], xr.at[0, d - 1], {"r": step_to(x, d)})
+
+        def over_came(d):
+            here = X.at[step_to(x, -d)]
+            return remote(here, here, xs.at[0, d - 1], xr.at[0, d - 1], {"r": step_to(x, d)})
+
+        def share(d):
+            return remote(G.at[x], G.at[x], xs.at[1, d - 1], xr.at[1, d - 1], {"r": step_to(x, d)})
+
+        def share_came(d):
+            here = G.at[step_to(x, -d)]
+            return remote(here, here, xs.at[1, d - 1], xr.at[1, d - 1], {"r": step_to(x, d)})
+
+        def store(q):
+            return pltpu.make_async_copy(G.at[q], out.at[:, pl.ds(q * C, C)], os.at[q])
 
         def e0():
-            pltpu.make_async_copy(part, F, ls).start()
-            pltpu.make_async_copy(part, F, ls).wait()
+            if held is None:
+                pltpu.make_async_copy(part, F, ls).start()
+                pltpu.make_async_copy(part, F, ls).wait()
             for r in rings:
                 r.first()
 
@@ -323,32 +347,57 @@
             for o, r in enumerate(rings):
 
                 def put(a, i, value, o=o):
-                    X[x, 2 * o + a] = value
+                    E[2 * o + a] = value
 
                 r.last(put)
+            X[x] = E[x]
 
         def e4():
-            for d in (1, 3, 2):
+            for d in (2, 1, 3):
                 over(d).start()
 
         def e5():
             for d in (1, 3, 2):
-                came(d).wait_recv()
+                over_came(d).wait_recv()
+            G[x] = added(*(X[i] for i in range(4)))
+
+        def e6():
+            for d in (2, 1, 3):
+                share(d).start()
+
+        def e7():
+            for d in (1, 3, 2):
+                share_came(d).wait_recv()
             for q in range(4):
-                done[:, q * C : (q + 1) * C] = added(*(X[i, q] for i in range(4)))
-
-        def e6():
-            pltpu.make_async_copy(done, out, os).start()
+                store(q).start()
             for r in rings:
                 r.drain()
             for d in (1, 3, 2):
                 over(d).wait_send()
-            pltpu.make_async_copy(done, out, os).wait()
-
-        return [e0, e1, e2, e3, e4, e5, e6]
-
-
-def run(name, number, steps, arrays, specs, outs, out_specs, compute, jobs=(), when=None, flops=0):
+                share(d).wait_send()
+            for q in range(4):
+                store(q).wait()
+
+        return [e0, e1, e2, e3, e4, e5, e6, e7]
+
+
+class Sum:
+    far = True
+
+    def __init__(self, grad):
+        self.a = SumA(grad)
+        self.b = SumB(None, (self.a.R, self.a.C))
+        self.inputs, self.outs, self.out_specs = self.a.inputs, self.b.outs, self.b.out_specs
+        self.scratch = self.a.scratch + self.b.scratch
+
+    def events(self, ins, outs, scratch):
+        n = len(self.a.scratch)
+        first = self.a.events(ins, [None], scratch[:n])
+        second = self.b.events([None], outs, scratch[n:], held=scratch[3])
+        return first[:-1] + second + first[-1:]
+
+
+def run(name, number, steps, arrays, specs, outs, out_specs, compute, jobs=(), when=None, flops=0, hold=(), order=None):
     n_in, n_out = len(arrays), len(outs)
     job_in = [a for j in jobs for a in j.inputs]
     job_out = [a for j in jobs for a in j.outs]
@@ -358,6 +407,7 @@
         jin, rest = rest[: len(job_in)], rest[len(job_in) :]
         mouts, rest = rest[:n_out], rest[n_out:]
         jout, scratch = rest[: len(job_out)], rest[len(job_out) :]
+        held, scratch = scratch[: len(hold)], scratch[len(hold) :]
         t = pl.program_id(0)
         lists = []
         for j in jobs:
@@ -392,13 +442,14 @@
                         e()
 
         if compute is not None:
-            compute(t, ins, mouts)
+            compute(t, ins, (*mouts, *held))
         if steps in table:
 
             @pl.when(t == steps - 1)
             def _():
-                for _, _, e in sorted(table[steps], key=lambda v: v[:2]):
-                    e()
+                late = {(i, j): e for i, j, e in table[steps]}
+                for key in [(i, j) for j, i in order] if order else sorted(late):
+                    late[key]()
 
     got = pl.pallas_call(
         body,
@@ -407,7 +458,7 @@
         out_shape=list(outs) + job_out,
         in_specs=list(specs) + [ANY] * len(job_in),
         out_specs=list(out_specs) + [s for j in jobs for s in j.out_specs],
-        scratch_shapes=[s for j in jobs for s in j.scratch],
+        scratch_shapes=list(hold) + [s for j in jobs for s in j.scratch],
         compiler_params=pltpu.CompilerParams(
             dimension_semantics=("arbitrary",),
             vmem_limit_bytes=66_000_000,
@@ -446,10 +497,10 @@
     return jax.ShapeDtypeStruct(dims, dtype)
 
 
-ROWS = 512
-
-
-def by_rows(total, fn):
+def by_rows(total, ROWS, fn):
+    if total == ROWS:
+        return fn(slice(None))
+
     def body(i, _):
         fn(pl.ds(pl.multiple_of(i * ROWS, ROWS), ROWS))
         return 0
@@ -467,7 +518,7 @@
         up_ref[rows, :] = up
         hid_ref[rows, :] = (gate * jax.nn.sigmoid(gate) * up).astype(BF)
 
-    by_rows(a.shape[0], part)
+    by_rows(a.shape[0], a.shape[0], part)
 
 
 def glu_back(by_hid, gate, up):
@@ -479,50 +530,58 @@
 
 def both_ways(t, ins, outs):
     a, dy, wg, wu, wd = ins
-    hid_ref, dg_ref, du_ref = outs
+    dg_ref, du_ref, gd_ref, hid_ref = outs
 
     def part(rows):
         gate, up = nn(a[rows, :], wg[...]), nn(a[rows, :], wu[...])
         hid_ref[rows, :], dg_ref[rows, :], du_ref[rows, :] = glu_back(nt(dy[rows, :], wd[...]), gate, up)
 
-    by_rows(a.shape[0], part)
+    by_rows(a.shape[0], 1024, part)
+    gd_ref[...] = tn(hid_ref[...], dy[...]).astype(BF)
 
 
 def back(t, ins, outs):
-    dy, wd, gate, up = ins
-    dg_ref, du_ref = outs
+    dy, wd, gate, up, hid = ins
+    dg_ref, du_ref, gd_ref = outs
 
     def part(rows):
         _, dg_ref[rows, :], du_ref[rows, :] = glu_back(nt(dy[rows, :], wd[...]), gate[rows, :], up[rows, :])
 
-    by_rows(dy.shape[0], part)
-
-
-def lower(t, ins, outs):
-    hid, wd, h = ins
-    outs[0][...] = h[...] + nn(hid[...], wd[...]).astype(BF)
-
-
-def grad_two(t, ins, outs):
-    at, dg, du = ins
-    outs[0][...] = nn(at[...], dg[...]).astype(BF)
-    outs[1][...] = nn(at[...], du[...]).astype(BF)
-
-
-def grad_down(t, ins, outs):
-    hid, dy = ins
-    outs[0][...] = tn(hid[...], dy[...]).astype(BF)
-
-
-def grad_a(t, ins, outs):
-    dg, du, wg, wu = ins
-    outs[0][...] = nt(dg[...], wg[...]).astype(BF) + nt(du[...], wu[...]).astype(BF)
+    by_rows(dy.shape[0], 512, part)
+    gd_ref[...] = tn(hid[...], dy[...]).astype(BF)
 
 
 def normed(h):
     wide = h.astype(F32)
     scale = lax.rsqrt(jnp.mean(wide**2, -1, keepdims=True) + 1e-6)
     return (wide * scale).astype(BF)
+
+
+def norm(t, ins, outs):
+    outs[0][...] = normed(ins[0][...])
+
+
+def lower(t, ins, outs):
+    hid, wd, h = ins
+    below = h[...] + nn(hid[...], wd[...]).astype(BF)
+    outs[0][...] = below
+    outs[1][...] = normed(below)
+
+
+def grad_two(t, ins, outs):
+    a, dg, du = ins
+    outs[0][...] = tn(a[...], dg[...]).astype(BF)
+    outs[1][...] = tn(a[...], du[...]).astype(BF)
+
+
+def grad_a(t, ins, outs):
+    dg, du, wg, wu, h, dy = ins
+    by_a = (nt(dg[...], wg[...]).astype(BF) + nt(du[...], wu[...]).astype(BF)).astype(F32)
+    wide = h[...].astype(F32)
+    scale = lax.rsqrt(jnp.mean(wide**2, -1, keepdims=True) + 1e-6)
+    along = jnp.mean(by_a * wide, -1, keepdims=True)
+    by_h = by_a * scale - wide * (along * scale * scale * scale)
+    outs[0][...] = dy[...] + by_h.astype(BF)
 
 
 def adamw(w, m, v, g):
@@ -535,58 +594,55 @@
 def solution(mesh):
     def step(x, dy, *arrays):
         (wg, wu, wd), m, v = (arrays[i : i + 3] for i in (0, 3, 6))
-        x, dy = x[0], dy[0]
-        N, D = x.shape
+        N, D = x.shape[1:]
         FF = wg.shape[2]
         B, TB = 256, 256
         T, TN = FF // B, N // TB
         one = 2 * N * D * FF
         flat = lambda w: w.reshape(-1, w.shape[-1])
-        tok, wide, ffd = (N, D), shape(N, FF), shape(FF, D)
-
-        wg1, wu1 = map(flat, run("fetch_0", 1, 1, [], [], [], [], None, [Gather(0, wg[0]), Gather(1, wu[0])], flops=one))
-        a1 = normed(x)
+        wide, tokens = shape(N, FF), shape(N, D)
+        whole = fixed((N, D))
+        raw_whole = pl.BlockSpec((None, N, D), lambda t: (0, 0, 0), pipeline_mode=pl.Buffered(1))
+        raw_rows = pl.BlockSpec((None, TB, D), lambda t: (0, t, 0))
+        rows = down_by(TB, D)
+
+        a1, wg1, wu1 = run("fetch_0", 1, TN, [x], [raw_rows], [tokens], [rows], norm, [Gather(0, wg[0]), Gather(1, wu[0])], [[0], [0]], one)
         gate1, up1, hid1, wd1, wg2 = run(
-            "glu_0", 2, T, [a1, wg1, wu1], [fixed(tok), across(D, B), across(D, B)],
+            "glu_0", 2, T, [a1, flat(wg1), flat(wu1)], [whole, across(D, B), across(D, B)],
             [shape(N, FF, dtype=F32), shape(N, FF, dtype=F32), wide], [across(N, B)] * 3, glu,
-            [Gather(0, wd[0]), Gather(1, wg[1])], [[0, 2, 4, 8, 12], [0, 2, 4, 8, 12]], 2 * one,
+            [Gather(0, wd[0]), Gather(1, wg[1])], [[0, 2, 3, 4, 6, 8, 11]] * 2, 2 * one,
         )
         wd1, wg2 = flat(wd1), flat(wg2)
-        h1, wu2, wd2 = run(
-            "lower_0", 3, TN, [hid1, wd1, x], [down_by(TB, FF), fixed((FF, D)), down_by(TB, D)],
-            [shape(N, D)], [down_by(TB, D)], lower,
-            [Gather(0, wu[1]), Gather(1, wd[1])], [[0, 2, 4], [0, 2, 4]], one,
+        h1, a2, wu2, wd2 = run(
+            "lower_0", 3, TN, [hid1, wd1, x], [down_by(TB, FF), fixed((FF, D)), raw_rows],
+            [tokens] * 2, [rows] * 2, lower, [Gather(0, wu[1]), Gather(1, wd[1])], [[0, 2, 3, 4, 5, 7]] * 2, one,
         )
         wu2, wd2 = flat(wu2), flat(wd2)
-        a2, back_norm = jax.vjp(normed, h1)
-        hid2, dg2, du2 = run(
-            "both_1", 0, T, [a2, dy, wg2, wu2, wd2], [fixed(tok), fixed(tok), across(D, B), across(D, B), down_by(B, D)],
-            [wide] * 3, [across(N, B)] * 3, both_ways, flops=3 * one,
+        dg2, du2, gd2 = run(
+            "both_1", 0, T, [a2, dy, wg2, wu2, wd2], [whole, raw_whole, across(D, B), across(D, B), down_by(B, D)],
+            [wide, wide, shape(FF, D)], [across(N, B)] * 2 + [down_by(B, D)], both_ways, flops=4 * one, hold=[pltpu.VMEM((N, B), BF)],
         )
-        (gd2,) = run("grad_down_1", 0, T, [hid2, dy], [across(N, B), fixed(tok)], [ffd], [down_by(B, D)], grad_down, flops=one)
         gg2, gu2, fd2 = run(
-            "grad_two_1", 4, T, [a2.T, dg2, du2], [fixed((D, N)), across(N, B), across(N, B)],
-            [shape(D, FF)] * 2, [across(D, B)] * 2, grad_two, [SumA(gd2)], [[0, 3, 4, 9, 10]], 2 * one,
+            "grad_two_1", 4, T, [a2, dg2, du2], [whole, across(N, B), across(N, B)],
+            [shape(D, FF)] * 2, [across(D, B)] * 2, grad_two, [SumA(gd2)], [[0, 3, 3, 8, 8, 11]], 2 * one,
         )
-        by_a, fg2, sd2 = run(
-            "grad_a_1", 5, TN, [dg2, du2, wg2, wu2], [down_by(TB, FF)] * 2 + [fixed((D, FF))] * 2,
-            [shape(N, D)], [down_by(TB, D)], grad_a, [SumA(gg2), SumB(fd2)], [[0, 2, 3, 6, 7], [0, 1, 2, 3, 4, 7]], 2 * one,
+        dh, fg2, sd2 = run(
+            "grad_a_1", 5, TN, [dg2, du2, wg2, wu2, h1, dy], [down_by(TB, FF)] * 2 + [fixed((D, FF))] * 2 + [rows, raw_rows],
+            [tokens], [rows], grad_a, [SumA(gg2), SumB(fd2)], [[0, 2, 2, 5, 5, 7], [0, 1, 1, 3, 3, 4, 4, 6]], 2 * one,
         )
-        dh = dy + back_norm(by_a)[0]
-        dg1, du1, fu2, sg2 = run(
-            "back_0", 6, T, [dh, wd1, gate1, up1], [fixed(tok), down_by(B, D), across(N, B), across(N, B)],
-            [wide] * 2, [across(N, B)] * 2, back, [SumA(gu2), SumB(fg2)], [[0, 3, 4, 9, 10], [0, 2, 3, 5, 6, 13]], one,
+        dg1, du1, gd1, fu2, sg2 = run(
+            "back_0", 6, T, [dh, wd1, gate1, up1, hid1], [whole, down_by(B, D)] + [across(N, B)] * 3,
+            [wide, wide, shape(FF, D)], [across(N, B)] * 2 + [down_by(B, D)], back,
+            [SumA(gu2), SumB(fg2)], [[0, 2, 2, 6, 6, 9, 11], [0, 1, 1, 3, 3, 5, 5, 8]], 2 * one,
         )
-        gd1, su2 = run(
-            "grad_down_0", 7, T, [hid1, dh], [across(N, B), fixed(tok)], [ffd], [down_by(B, D)], grad_down,
-            [SumB(fu2)], [[0, 3, 4, 6, 7, 13]], one,
+        gg1, gu1, fd1, su2 = run(
+            "grad_two_0", 7, T, [a1, dg1, du1], [whole, across(N, B), across(N, B)],
+            [shape(D, FF)] * 2, [across(D, B)] * 2, grad_two, [SumA(gd1), SumB(fu2)], [[0, 3, 3, 8, 8, 11], [0, 2, 2, 5, 5, 7, 7, 10]], 2 * one,
         )
-        gg1, gu1, fd1 = run(
-            "grad_two_0", 8, T, [a1.T, dg1, du1], [fixed((D, N)), across(N, B), across(N, B)],
-            [shape(D, FF)] * 2, [across(D, B)] * 2, grad_two, [SumA(gd1)], [[0, 3, 4, 9, 10]], 2 * one,
-        )
-        fg1, fu1, sd1 = run("sum_a", 9, 1, [], [], [], [], None, [SumA(gg1), SumA(gu1), SumB(fd1)], flops=one)
-        sg1, su1 = run("sum_b", 10, 1, [], [], [], [], None, [SumB(fg1), SumB(fu1)], flops=one)
+        order = [(0, 0), (1, 0), (2, 0), (0, 1), (0, 2), (2, 1), (2, 2), (1, 1), (1, 2), (2, 3), (2, 4), (0, 3), (0, 4), (2, 5), (2, 6)]
+        order += [(1, 3), (1, 4), (0, 5), (0, 6), (1, 5), (1, 6), (2, 7), (0, 7), (0, 8), (1, 7), (1, 8), (0, 9), (0, 10), (1, 9), (1, 10)]
+        order += [(0, 11), (0, 12), (1, 11), (1, 12), (0, 13), (1, 13), (0, 14), (1, 14)]
+        sg1, su1, sd1 = run("sum_last", 8, 1, [], [], [], [], None, [Sum(gg1), Sum(gu1), SumB(fd1)], flops=one, order=order)
 
         sums = [(sg1, sg2), (su1, su2), (sd1, sd2)]
         gradients = [jnp.stack(pair).astype(F32) for pair in sums]

time: 630 us -> 518 us (0.82)
  Pallas kernels: 557 us -> 504 us
  other arithmetic: 45.6 us -> 8.41 us
  local copies, waits for them, and re-layouts: 23 us -> 4.09 us
    pallas_call x12 -> x9, Pallas kernels: 557 us -> 504 us  [run(): pl.pallas_call(body, name=name, grid=(steps,), out_shape=list(outs) + job...]
    reduce_sum x3 -> x0, other arithmetic: 10.9 us -> none  [the longest x2 6.14 us: normed(): scale = lax.rsqrt(jnp.mean(wide ** 2, -1, keepdims=True) + 1e-06)]
    convert_element_type x2 -> x0, other arithmetic: 10.6 us -> none  [normed(): return (wide * scale).astype(BF)]
    transpose x2 -> x0, other arithmetic: 10.5 us -> none  [the longest x1 5.49 us: step(): gg1, gu1, fd1 = run('grad_two_0', 8, T, [a1.T, dg1, du1], [fixed((D, N)),...]
    unnamed x29 -> x14, local copies, waits for them, and re-layouts: 8.32 us -> 0.04 us
    transpose x1 -> x0, local copies, waits for them, and re-layouts: 6.55 us -> none  [step(): gg2, gu2, fd2 = run('grad_two_1', 4, T, [a2.T, dg2, du2], [fixed((D, N)),...]
    convert_element_type x1 -> x0, local copies, waits for them, and re-layouts: 6.39 us -> none  [normed(): return (wide * scale).astype(BF)]
where the time goes in v2:
time: 518 us
  Pallas kernels  504 us (97%)
  other arithmetic  8.41 us (2%)
    pallas_call x9, Pallas kernels, run(): pl.pallas_call(body, name=name, grid=(steps,), out_shape=list(outs) + job...  504 us

profile of v2, /device:TPU:1, one launch (start us, length us, event | category | flops | bytes accessed | tf_op | source)
XLA Modules:
  0.0 517.5 jit_solution(16652815283567528229)
XLA Ops:
  0.6 1.8 slice_bitcast_fusion
  2.5 2.2 slice_bitcast_fusion.1
  4.7 51.9 %fetch_0.1 = (bf16[2048,1024]{1,0:T(8,128)(2,1)}, bf16[4,4,2,32,3584]{4,3,2,1,0:T(8,128)(2,1)}, bf16[4,4,2,32,3584]{4,3,2,1,0:T(8,128)(2,1)}) custom-call(bf16[1,2048,1024]{2,1,0:T(8,128)(2,1)} %refs_2_.1, bf16[32,3584]{1,0:T(8,128)(2,1)} %get-tuple-element.90.refs_1_, bf16[32,3584]{1,0:T(8,128)(2,1)} %get-tuple-element.87.refs_2_), custom_call_target="tpu_custom_call" | custom-call | flops 15032385536 | bytes 50000000 | tf_op jit(solution)/shard_map/fetch_0/pallas_call | solution.py:454
  56.6 58.4 %glu_0.1 = (f32[2048,3584]{1,0:T(8,128)}, f32[2048,3584]{1,0:T(8,128)}, bf16[2048,3584]{1,0:T(8,128)(2,1)}, bf16[4,4,2,112,1024]{4,3,2,1,0:T(8,128)(2,1)}, bf16[4,4,2,32,3584]{4,3,2,1,0:T(8,128)(2,1)}) custom-call(bf16[2048,1024]{1,0:T(8,128)(2,1)} %get-tuple-element.42.refs_0_, bf16[1024,3584]{1,0:T(8,128)(2,1)} %bitcast.45, bf16[1024,3584]{1,0:T(8,128)(2,1)} %bitcast.46, ...), custom_call_target="tpu_custom_call" | custom-call | flops 30064771072 | bytes 50000000 | tf_op jit(solution)/shard_map/glu_0/pallas_call | solution.py:454
  115.0 50.4 %lower_0.1 = (bf16[2048,1024]{1,0:T(8,128)(2,1)}, bf16[2048,1024]{1,0:T(8,128)(2,1)}, bf16[4,4,2,32,3584]{4,3,2,1,0:T(8,128)(2,1)}, bf16[4,4,2,112,1024]{4,3,2,1,0:T(8,128)(2,1)}) custom-call(bf16[2048,3584]{1,0:T(8,128)(2,1)} %get-tuple-element.45.refs_0_.refs_4_, bf16[3584,1024]{1,0:T(8,128)(2,1)} %bitcast.36, bf16[1,2048,1024]{2,1,0:T(8,128)(2,1)} %refs_2_.1, ...), custom_call_target="tpu_custom_call" | custom-call | flops 15032385536 | bytes 50000000 | tf_op jit(solution)/shard_map/lower_0/pallas_call | solution.py:454
  165.5 75.3 %both_1.1 = (bf16[2048,3584]{1,0:T(8,128)(2,1)}, bf16[2048,3584]{1,0:T(8,128)(2,1)}, bf16[3584,1024]{1,0:T(8,128)(2,1)}) custom-call(bf16[2048,1024]{1,0:T(8,128)(2,1)} %get-tuple-element.47.refs_0_, bf16[1,2048,1024]{2,1,0:T(8,128)(2,1)} %refs_5_.1, bf16[1024,3584]{1,0:T(8,128)(2,1)} %bitcast.38, bf16[1024,3584]{1,0:T(8,128)(2,1)} %bitcast.41, ...), custom_call_target="tpu_custom_call" | custom-call | flops 60129542144 | bytes 50000000 | tf_op jit(solution)/shard_map/both_1/pallas_call | solution.py:454
  240.7 42.4 %grad_two_1.1 = (bf16[1024,3584]{1,0:T(8,128)(2,1)}, bf16[1024,3584]{1,0:T(8,128)(2,1)}, bf16[2,2,4,112,256]{4,3,2,1,0:T(8,128)(2,1)}) custom-call(bf16[2048,1024]{1,0:T(8,128)(2,1)} %get-tuple-element.47.refs_0_, bf16[2048,3584]{1,0:T(8,128)(2,1)} %get-tuple-element.51.refs_1_.refs_0_, bf16[2048,3584]{1,0:T(8,128)(2,1)} %get-tuple-element.52.refs_2_.refs_1_, ...), custom_call_target="tpu_custom_call" | custom-call | flops 30064771072 | bytes 50000000 | tf_op jit(solution)/shard_map/grad_two_1/pallas_call | solution.py:454
  283.1 51.6 %grad_a_1.1 = (bf16[2048,1024]{1,0:T(8,128)(2,1)}, bf16[2,2,4,32,896]{4,3,2,1,0:T(8,128)(2,1)}, bf16[112,1024]{1,0:T(8,128)(2,1)}) custom-call(bf16[2048,3584]{1,0:T(8,128)(2,1)} %get-tuple-element.51.refs_1_.refs_0_, bf16[2048,3584]{1,0:T(8,128)(2,1)} %get-tuple-element.52.refs_2_.refs_1_, bf16[1024,3584]{1,0:T(8,128)(2,1)} %bitcast.39, ...), custom_call_target="tpu_custom_call" | custom-call | flops 30064771072 | bytes 50000000 | tf_op jit(solution)/shard_map/grad_a_1/pallas_call | solution.py:454
  334.8 64.5 %back_0.1 = (bf16[2048,3584]{1,0:T(8,128)(2,1)}, bf16[2048,3584]{1,0:T(8,128)(2,1)}, bf16[3584,1024]{1,0:T(8,128)(2,1)}, bf16[2,2,4,32,896]{4,3,2,1,0:T(8,128)(2,1)}, bf16[32,3584]{1,0:T(8,128)(2,1)}) custom-call(bf16[2048,1024]{1,0:T(8,128)(2,1)} %get-tuple-element.57.refs_0_, bf16[3584,1024]{1,0:T(8,128)(2,1)} %bitcast.37, ...), custom_call_target="tpu_custom_call" | custom-call | flops 30064771072 | bytes 50000000 | tf_op jit(solution)/shard_map/back_0/pallas_call | solution.py:454
  399.2 47.1 %grad_two_0.1 = (bf16[1024,3584]{1,0:T(8,128)(2,1)}, bf16[1024,3584]{1,0:T(8,128)(2,1)}, bf16[2,2,4,112,256]{4,3,2,1,0:T(8,128)(2,1)}, bf16[32,3584]{1,0:T(8,128)(2,1)}) custom-call(bf16[2048,1024]{1,0:T(8,128)(2,1)} %get-tuple-element.42.refs_0_, bf16[2048,3584]{1,0:T(8,128)(2,1)} %get-tuple-element.62.refs_1_, ...), custom_call_target="tpu_custom_call" | custom-call | flops 30064771072 | bytes 50000000 | tf_op jit(solution)/shard_map/grad_two_0/pallas_call | solution.py:454
  446.3 0.0 copy-start
  446.3 0.0 copy-start.1
  446.3 62.7 %sum_last.1 = (bf16[32,3584]{1,0:T(8,128)(2,1)}, bf16[32,3584]{1,0:T(8,128)(2,1)}, bf16[112,1024]{1,0:T(8,128)(2,1)}) custom-call(bf16[4,4,2,32,3584]{4,3,2,1,0:T(8,128)(2,1)} %bitcast.47, bf16[4,4,2,32,3584]{4,3,2,1,0:T(8,128)(2,1)} %bitcast.48, bf16[2,2,4,112,256]{4,3,2,1,0:T(8,128)(2,1)} %get-tuple-element.68.refs_2_), custom_call_target="tpu_custom_call" | custom-call | flops 15032385536 | bytes 50000000 | tf_op jit(solution)/shard_map/sum_last/pallas_call | solution.py:454
  509.0 0.0 copy-start.2
  509.0 0.0 copy-start.3
  509.0 0.0 copy-start.4
  509.1 0.0 copy-start.5
  509.1 0.0 copy-start.6
  509.1 0.0 copy-done
  509.1 3.4 fusion.6
  512.5 0.0 copy-done.1
  512.5 3.3 fusion.2
  515.8 0.0 copy-done.2
  515.9 1.7 fusion.10
  (4 shorter events, 0.0 us)
Async XLA Ops:
  446.3 62.8 %copy-start = (bf16[2,32,3584]{2,1,0:T(8,128)(2,1)S(1)}, bf16[2,32,3584]{2,1,0:T(8,128)(2,1)}, u32[]{:S(2)}) copy-start(bf16[2,32,3584]{2,1,0:T(8,128)(2,1)} %param.14) | copy-start | bytes 1376260
  446.3 66.2 %copy-start.1 = (bf16[2,32,3584]{2,1,0:T(8,128)(2,1)S(1)}, bf16[2,32,3584]{2,1,0:T(8,128)(2,1)}, u32[]{:S(2)}) copy-start(bf16[2,32,3584]{2,1,0:T(8,128)(2,1)} %param.13) | copy-start | bytes 1376260
  509.0 6.8 %copy-start.2 = (bf16[2,112,1024]{2,1,0:T(8,128)(2,1)S(1)}, bf16[2,112,1024]{2,1,0:T(8,128)(2,1)}, u32[]{:S(2)}) copy-start(bf16[2,112,1024]{2,1,0:T(8,128)(2,1)} %param.15) | copy-start | bytes 1376260
  509.0 6.8 %copy-start.3 = (f32[2,112,1024]{2,1,0:T(8,128)S(1)}, f32[2,112,1024]{2,1,0:T(8,128)}, u32[]{:S(2)}) copy-start(f32[2,112,1024]{2,1,0:T(8,128)} %param.21) | copy-start | bytes 2752516
  509.0 6.8 %copy-start.4 = (f32[2,112,1024]{2,1,0:T(8,128)S(1)}, f32[2,112,1024]{2,1,0:T(8,128)}, u32[]{:S(2)}) copy-start(f32[2,112,1024]{2,1,0:T(8,128)} %param.18) | copy-start | bytes 2752516
  509.1 6.8 %copy-start.5 = (bf16[112,1024]{1,0:T(8,128)(2,1)S(1)}, bf16[112,1024]{1,0:T(8,128)(2,1)}, u32[]{:S(2)}) copy-start(bf16[112,1024]{1,0:T(8,128)(2,1)} %get-tuple-element.74) | copy-start | bytes 688132
  509.1 6.8 %copy-start.6 = (bf16[112,1024]{1,0:T(8,128)(2,1)S(1)}, bf16[112,1024]{1,0:T(8,128)(2,1)}, u32[]{:S(2)}) copy-start(bf16[112,1024]{1,0:T(8,128)(2,1)} %get-tuple-element.73) | copy-start | bytes 688132

commit v3 on v2

--- a/solution.py
+++ b/solution.py
@@ -42,19 +42,20 @@
 
 
 class Gather:
-    far = False
-
-    def __init__(self, order, shard):
-        self.order = order
-        rows, cols = shard.shape
+    far, pair = False, 0
+
+    def __init__(self, order, shards, layer):
+        self.order, self.layer = order, layer
+        _, rows, cols = shards.shape
         self.rows, self.cols = rows, cols
-        self.inputs = [shard]
+        self.inputs = [shards]
         self.outs = [jax.ShapeDtypeStruct((4, 4, 2, rows, cols), BF)]
         self.out_specs = [ANY]
         self.scratch = [pltpu.VMEM((rows, cols), BF), pltpu.SemaphoreType.DMA((27,)), pltpu.SemaphoreType.DMA((27,)), pltpu.SemaphoreType.DMA((2,))]
 
     def events(self, ins, outs, scratch):
         (own,), (full,) = ins, outs
+        own = own.at[self.layer]
         hold, ss, rs, local = scratch
         o, half = self.order, self.cols // 2
         _, y, z, c = place()
@@ -206,7 +207,7 @@
 
 
 class SumA:
-    far = False
+    far, pair = False, 1
 
     def __init__(self, grad):
         rows, cols = grad.shape
@@ -287,7 +288,7 @@
 
 
 class SumB:
-    far = True
+    far, pair = True, 1
 
     def __init__(self, part, dims=None):
         R, C = dims or part.shape[3:]
@@ -382,7 +383,7 @@
 
 
 class Sum:
-    far = True
+    far, pair = True, 1
 
     def __init__(self, grad):
         self.a = SumA(grad)
@@ -397,7 +398,7 @@
         return first[:-1] + second + first[-1:]
 
 
-def run(name, number, steps, arrays, specs, outs, out_specs, compute, jobs=(), when=None, flops=0, hold=(), order=None):
+def run(name, number, steps, arrays, specs, outs, out_specs, compute, jobs=(), when=None, flops=0, hold=()):
     n_in, n_out = len(arrays), len(outs)
     job_in = [a for j in jobs for a in j.inputs]
     job_out = [a for j in jobs for a in j.outs]
@@ -428,17 +429,22 @@
                     pl.semaphore_signal(barrier, inc=1, device_id=device, device_id_type=MESH)
                 pl.semaphore_wait(barrier, len(them))
 
+        def turn(entry):
+            i, j, _ = entry
+            pair = jobs[j].pair
+            return (i + pair) // (1 + pair), j, i
+
         table = {}
         for j, events in enumerate(lists):
             for i, e in enumerate(events):
-                at = when[j][i] if when and i < len(when[j]) else steps
+                at = int(when[j][i], 36) if when and i < len(when[j]) else steps
                 table.setdefault(min(at, steps), []).append((i, j, e))
         for at in sorted(table):
             if at < steps:
 
                 @pl.when(t == at)
                 def _(at=at):
-                    for _, _, e in sorted(table[at], key=lambda v: v[:2]):
+                    for _, _, e in sorted(table[at], key=turn):
                         e()
 
         if compute is not None:
@@ -447,9 +453,8 @@
 
             @pl.when(t == steps - 1)
             def _():
-                late = {(i, j): e for i, j, e in table[steps]}
-                for key in [(i, j) for j, i in order] if order else sorted(late):
-                    late[key]()
+                for _, _, e in sorted(table[steps], key=turn):
+                    e()
 
     got = pl.pallas_call(
         body,
@@ -511,14 +516,10 @@
 def glu(t, ins, outs):
     a, wg, wu = ins
     gate_ref, up_ref, hid_ref = outs
-
-    def part(rows):
-        gate, up = nn(a[rows, :], wg[...]), nn(a[rows, :], wu[...])
-        gate_ref[rows, :] = gate
-        up_ref[rows, :] = up
-        hid_ref[rows, :] = (gate * jax.nn.sigmoid(gate) * up).astype(BF)
-
-    by_rows(a.shape[0], a.shape[0], part)
+    gate, up = nn(a[...], wg[...]), nn(a[...], wu[...])
+    gate_ref[...] = gate
+    up_ref[...] = up
+    hid_ref[...] = (gate * jax.nn.sigmoid(gate) * up).astype(BF)
 
 
 def glu_back(by_hid, gate, up):
@@ -606,16 +607,16 @@
         raw_rows = pl.BlockSpec((None, TB, D), lambda t: (0, t, 0))
         rows = down_by(TB, D)
 
-        a1, wg1, wu1 = run("fetch_0", 1, TN, [x], [raw_rows], [tokens], [rows], norm, [Gather(0, wg[0]), Gather(1, wu[0])], [[0], [0]], one)
+        a1, wg1, wu1 = run("fetch_0", 1, TN, [x], [raw_rows], [tokens], [rows], norm, [Gather(0, wg, 0), Gather(1, wu, 0)], ["0", "0"], one)
         gate1, up1, hid1, wd1, wg2 = run(
             "glu_0", 2, T, [a1, flat(wg1), flat(wu1)], [whole, across(D, B), across(D, B)],
             [shape(N, FF, dtype=F32), shape(N, FF, dtype=F32), wide], [across(N, B)] * 3, glu,
-            [Gather(0, wd[0]), Gather(1, wg[1])], [[0, 2, 3, 4, 6, 8, 11]] * 2, 2 * one,
+            [Gather(0, wd, 0), Gather(1, wg, 1)], ["024579c"] * 2, 2 * one,
         )
         wd1, wg2 = flat(wd1), flat(wg2)
         h1, a2, wu2, wd2 = run(
             "lower_0", 3, TN, [hid1, wd1, x], [down_by(TB, FF), fixed((FF, D)), raw_rows],
-            [tokens] * 2, [rows] * 2, lower, [Gather(0, wu[1]), Gather(1, wd[1])], [[0, 2, 3, 4, 5, 7]] * 2, one,
+            [tokens] * 2, [rows] * 2, lower, [Gather(0, wu, 1), Gather(1, wd, 1)], ["023457"] * 2, one,
         )
         wu2, wd2 = flat(wu2), flat(wd2)
         dg2, du2, gd2 = run(
@@ -624,25 +625,22 @@
         )
         gg2, gu2, fd2 = run(
             "grad_two_1", 4, T, [a2, dg2, du2], [whole, across(N, B), across(N, B)],
-            [shape(D, FF)] * 2, [across(D, B)] * 2, grad_two, [SumA(gd2)], [[0, 3, 3, 8, 8, 11]], 2 * one,
+            [shape(D, FF)] * 2, [across(D, B)] * 2, grad_two, [SumA(gd2)], ["03388b"], 2 * one,
         )
         dh, fg2, sd2 = run(
             "grad_a_1", 5, TN, [dg2, du2, wg2, wu2, h1, dy], [down_by(TB, FF)] * 2 + [fixed((D, FF))] * 2 + [rows, raw_rows],
-            [tokens], [rows], grad_a, [SumA(gg2), SumB(fd2)], [[0, 2, 2, 5, 5, 7], [0, 1, 1, 3, 3, 4, 4, 6]], 2 * one,
+            [tokens], [rows], grad_a, [SumA(gg2), SumB(fd2)], ["022557", "01133446"], 2 * one,
         )
         dg1, du1, gd1, fu2, sg2 = run(
             "back_0", 6, T, [dh, wd1, gate1, up1, hid1], [whole, down_by(B, D)] + [across(N, B)] * 3,
             [wide, wide, shape(FF, D)], [across(N, B)] * 2 + [down_by(B, D)], back,
-            [SumA(gu2), SumB(fg2)], [[0, 2, 2, 6, 6, 9, 11], [0, 1, 1, 3, 3, 5, 5, 8]], 2 * one,
+            [SumA(gu2), SumB(fg2)], ["022669b", "01133558"], 2 * one,
         )
         gg1, gu1, fd1, su2 = run(
             "grad_two_0", 7, T, [a1, dg1, du1], [whole, across(N, B), across(N, B)],
-            [shape(D, FF)] * 2, [across(D, B)] * 2, grad_two, [SumA(gd1), SumB(fu2)], [[0, 3, 3, 8, 8, 11], [0, 2, 2, 5, 5, 7, 7, 10]], 2 * one,
+            [shape(D, FF)] * 2, [across(D, B)] * 2, grad_two, [SumA(gd1), SumB(fu2)], ["03388b", "0225577a"], 2 * one,
         )
-        order = [(0, 0), (1, 0), (2, 0), (0, 1), (0, 2), (2, 1), (2, 2), (1, 1), (1, 2), (2, 3), (2, 4), (0, 3), (0, 4), (2, 5), (2, 6)]
-        order += [(1, 3), (1, 4), (0, 5), (0, 6), (1, 5), (1, 6), (2, 7), (0, 7), (0, 8), (1, 7), (1, 8), (0, 9), (0, 10), (1, 9), (1, 10)]
-        order += [(0, 11), (0, 12), (1, 11), (1, 12), (0, 13), (1, 13), (0, 14), (1, 14)]
-        sg1, su1, sd1 = run("sum_last", 8, 1, [], [], [], [], None, [Sum(gg1), Sum(gu1), SumB(fd1)], flops=one, order=order)
+        sg1, su1, sd1 = run("sum_last", 8, 1, [], [], [], [], None, [Sum(gg1), Sum(gu1), SumB(fd1)], flops=one)
 
         sums = [(sg1, sg2), (su1, su2), (sd1, sd2)]
         gradients = [jnp.stack(pair).astype(F32) for pair in sums]

time: 518 us -> 511 us (0.986)
  no operation moved by 1% of the time
where the time goes in v3:
time: 511 us; the launch traced here: 510 us
  Pallas kernels  501 us (98%)
  other arithmetic  8.4 us (2%)
    pallas_call x9, Pallas kernels, run(): pl.pallas_call(body, name=name, grid=(steps,), out_shape=list(outs) + job...  501 us

profile of v3, /device:TPU:1, one launch (start us, length us, event | category | flops | bytes accessed | tf_op | source)
XLA Modules:
  0.0 510.4 jit_solution(5713049235292505182)
XLA Ops:
  0.6 52.0 %fetch_0.1 = (bf16[2048,1024]{1,0:T(8,128)(2,1)}, bf16[4,4,2,32,3584]{4,3,2,1,0:T(8,128)(2,1)}, bf16[4,4,2,32,3584]{4,3,2,1,0:T(8,128)(2,1)}) custom-call(bf16[1,2048,1024]{2,1,0:T(8,128)(2,1)} %refs_2_.3, bf16[2,32,3584]{2,1,0:T(8,128)(2,1)} %refs_4_.2, bf16[2,32,3584]{2,1,0:T(8,128)(2,1)} %refs_3_.3), custom_call_target="tpu_custom_call" | custom-call | flops 15032385536 | bytes 50000000 | tf_op jit(solution)/shard_map/fetch_0/pallas_call | solution.py:459
  52.7 55.7 %glu_0.1 = (f32[2048,3584]{1,0:T(8,128)}, f32[2048,3584]{1,0:T(8,128)}, bf16[2048,3584]{1,0:T(8,128)(2,1)}, bf16[4,4,2,112,1024]{4,3,2,1,0:T(8,128)(2,1)}, bf16[4,4,2,32,3584]{4,3,2,1,0:T(8,128)(2,1)}) custom-call(bf16[2048,1024]{1,0:T(8,128)(2,1)} %get-tuple-element.42.refs_0_, bf16[1024,3584]{1,0:T(8,128)(2,1)} %bitcast.35, bf16[1024,3584]{1,0:T(8,128)(2,1)} %bitcast.36, ...), custom_call_target="tpu_custom_call" | custom-call | flops 30064771072 | bytes 50000000 | tf_op jit(solution)/shard_map/glu_0/pallas_call | solution.py:459
  108.4 50.4 %lower_0.1 = (bf16[2048,1024]{1,0:T(8,128)(2,1)}, bf16[2048,1024]{1,0:T(8,128)(2,1)}, bf16[4,4,2,32,3584]{4,3,2,1,0:T(8,128)(2,1)}, bf16[4,4,2,112,1024]{4,3,2,1,0:T(8,128)(2,1)}) custom-call(bf16[2048,3584]{1,0:T(8,128)(2,1)} %get-tuple-element.45.refs_0_.refs_4_, bf16[3584,1024]{1,0:T(8,128)(2,1)} %bitcast.24, bf16[1,2048,1024]{2,1,0:T(8,128)(2,1)} %refs_2_.3, ...), custom_call_target="tpu_custom_call" | custom-call | flops 15032385536 | bytes 50000000 | tf_op jit(solution)/shard_map/lower_0/pallas_call | solution.py:459
  158.8 75.3 %both_1.1 = (bf16[2048,3584]{1,0:T(8,128)(2,1)}, bf16[2048,3584]{1,0:T(8,128)(2,1)}, bf16[3584,1024]{1,0:T(8,128)(2,1)}) custom-call(bf16[2048,1024]{1,0:T(8,128)(2,1)} %get-tuple-element.47.refs_0_, bf16[1,2048,1024]{2,1,0:T(8,128)(2,1)} %refs_5_.1, bf16[1024,3584]{1,0:T(8,128)(2,1)} %bitcast.26, bf16[1024,3584]{1,0:T(8,128)(2,1)} %bitcast.29, ...), custom_call_target="tpu_custom_call" | custom-call | flops 60129542144 | bytes 50000000 | tf_op jit(solution)/shard_map/both_1/pallas_call | solution.py:459
  234.1 42.3 %grad_two_1.1 = (bf16[1024,3584]{1,0:T(8,128)(2,1)}, bf16[1024,3584]{1,0:T(8,128)(2,1)}, bf16[2,2,4,112,256]{4,3,2,1,0:T(8,128)(2,1)}) custom-call(bf16[2048,1024]{1,0:T(8,128)(2,1)} %get-tuple-element.47.refs_0_, bf16[2048,3584]{1,0:T(8,128)(2,1)} %get-tuple-element.51.refs_1_.refs_0_, bf16[2048,3584]{1,0:T(8,128)(2,1)} %get-tuple-element.52.refs_2_.refs_1_, ...), custom_call_target="tpu_custom_call" | custom-call | flops 30064771072 | bytes 50000000 | tf_op jit(solution)/shard_map/grad_two_1/pallas_call | solution.py:459
  276.4 51.7 %grad_a_1.1 = (bf16[2048,1024]{1,0:T(8,128)(2,1)}, bf16[2,2,4,32,896]{4,3,2,1,0:T(8,128)(2,1)}, bf16[112,1024]{1,0:T(8,128)(2,1)}) custom-call(bf16[2048,3584]{1,0:T(8,128)(2,1)} %get-tuple-element.51.refs_1_.refs_0_, bf16[2048,3584]{1,0:T(8,128)(2,1)} %get-tuple-element.52.refs_2_.refs_1_, bf16[1024,3584]{1,0:T(8,128)(2,1)} %bitcast.27, ...), custom_call_target="tpu_custom_call" | custom-call | flops 30064771072 | bytes 50000000 | tf_op jit(solution)/shard_map/grad_a_1/pallas_call | solution.py:459
  328.1 64.4 %back_0.1 = (bf16[2048,3584]{1,0:T(8,128)(2,1)}, bf16[2048,3584]{1,0:T(8,128)(2,1)}, bf16[3584,1024]{1,0:T(8,128)(2,1)}, bf16[2,2,4,32,896]{4,3,2,1,0:T(8,128)(2,1)}, bf16[32,3584]{1,0:T(8,128)(2,1)}) custom-call(bf16[2048,1024]{1,0:T(8,128)(2,1)} %get-tuple-element.57.refs_0_, bf16[3584,1024]{1,0:T(8,128)(2,1)} %bitcast.25, ...), custom_call_target="tpu_custom_call" | custom-call | flops 30064771072 | bytes 50000000 | tf_op jit(solution)/shard_map/back_0/pallas_call | solution.py:459
  392.5 47.0 %grad_two_0.1 = (bf16[1024,3584]{1,0:T(8,128)(2,1)}, bf16[1024,3584]{1,0:T(8,128)(2,1)}, bf16[2,2,4,112,256]{4,3,2,1,0:T(8,128)(2,1)}, bf16[32,3584]{1,0:T(8,128)(2,1)}) custom-call(bf16[2048,1024]{1,0:T(8,128)(2,1)} %get-tuple-element.42.refs_0_, bf16[2048,3584]{1,0:T(8,128)(2,1)} %get-tuple-element.62.refs_1_, ...), custom_call_target="tpu_custom_call" | custom-call | flops 30064771072 | bytes 50000000 | tf_op jit(solution)/shard_map/grad_two_0/pallas_call | solution.py:459
  439.6 0.0 copy-start
  439.6 62.4 %sum_last.1 = (bf16[32,3584]{1,0:T(8,128)(2,1)}, bf16[32,3584]{1,0:T(8,128)(2,1)}, bf16[112,1024]{1,0:T(8,128)(2,1)}) custom-call(bf16[4,4,2,32,3584]{4,3,2,1,0:T(8,128)(2,1)} %bitcast.33, bf16[4,4,2,32,3584]{4,3,2,1,0:T(8,128)(2,1)} %bitcast.34, bf16[2,2,4,112,256]{4,3,2,1,0:T(8,128)(2,1)} %get-tuple-element.68.refs_2_), custom_call_target="tpu_custom_call" | custom-call | flops 15032385536 | bytes 50000000 | tf_op jit(solution)/shard_map/sum_last/pallas_call | solution.py:459
  502.0 3.5 fusion.10
  505.5 0.0 copy-done
  505.5 4.9 fusion.2
Async XLA Ops:
  439.6 65.9 %copy-start = (f32[2,32,3584]{2,1,0:T(8,128)S(1)}, f32[2,32,3584]{2,1,0:T(8,128)}, u32[]{:S(2)}) copy-start(f32[2,32,3584]{2,1,0:T(8,128)} %param.19) | copy-start | bytes 2752516
